TPU v7x, 8 devices: a whole 2x2x1 slice. The times are simulated.
8 devices in a mesh: dp: 2 (over z, y), tp: 4 (over x, core).
Axes of the slice: x: 2, y: 2, z: 1, core: 2. Of those that a mesh axis runs over, the one named last changes fastest.
Arguments:
- x: bfloat16 [2, 2048, 2560], P('dp', 'tp'), parts along dimension 0
- ln_gain: bfloat16 [2, 2560], replicated
- ln_bias: bfloat16 [2, 2560], replicated
- w_q: bfloat16 [2, 2560, 32, 80], P(None, None, 'tp')
- b_q: bfloat16 [2, 32, 80], P(None, 'tp')
- w_k: bfloat16 [2, 2560, 32, 80], P(None, None, 'tp')
- b_k: bfloat16 [2, 32, 80], P(None, 'tp')
- w_v: bfloat16 [2, 2560, 32, 80], P(None, None, 'tp')
- b_v: bfloat16 [2, 32, 80], P(None, 'tp')
- w_o: bfloat16 [2, 32, 80, 2560], P(None, 'tp')
- b_o: bfloat16 [2, 2560], replicated
- w_up: bfloat16 [2, 2560, 10240], P(None, None, 'tp')
- b_up: bfloat16 [2, 10240], P(None, 'tp')
- w_down: bfloat16 [2, 10240, 2560], P(None, 'tp')
- b_down: bfloat16 [2, 2560], replicated
Outputs:
- output: bfloat16 [2, 2048, 2560], P('dp', 'tp'), parts along dimension 0
There are 2 independent parts. A program takes and returns all parts, laid end to end along the dimension named above; an argument that names none is the same for every part.
All inputs are finite; a program needn't handle non-finite values.
Results may differ from a plain program's by a relative error of at most 0.0153974.
Values are sent between devices in bfloat16 or wider.
A program may use at most 1 GiB of HBM per device.

v0:
```python
import jax
import jax.numpy as jnp
from jax import lax
from jax.sharding import PartitionSpec as P

ROT_DIM = 32
ROPE_BASE = 10000.0
LN_EPS = 1e-5


def rotary_tables(seq_len):
    half = ROT_DIM // 2
    inv_freq = 1.0 / (ROPE_BASE ** (jnp.arange(half, dtype=jnp.float32) * (2.0 / ROT_DIM)))
    angles = jnp.arange(seq_len, dtype=jnp.float32)[:, None] * inv_freq[None, :]
    return jnp.cos(angles), jnp.sin(angles)


def apply_rotary(projected, cosine, sine):
    half = ROT_DIM // 2
    first = projected[..., :half]
    second = projected[..., half:ROT_DIM]
    return jnp.concatenate([first * cosine - second * sine, second * cosine + first * sine, projected[..., ROT_DIM:]], axis=-1)


def layer_norm(hidden, gain, bias):
    x_f32 = hidden.astype(jnp.float32)
    mean = jnp.mean(x_f32, axis=-1, keepdims=True)
    centered = x_f32 - mean
    variance = jnp.mean(centered * centered, axis=-1, keepdims=True)
    return (centered * lax.rsqrt(variance + LN_EPS) * gain.astype(jnp.float32) + bias.astype(jnp.float32)).astype(jnp.bfloat16)


def causal_attention(q_rot, k_rot, values):
    seq_len = q_rot.shape[2]
    head_dim = q_rot.shape[3]
    scores = jnp.einsum("bhqe,bhke->bhqk", q_rot, k_rot, preferred_element_type=jnp.float32) * (head_dim ** -0.5)
    causal = jnp.arange(seq_len)[:, None] >= jnp.arange(seq_len)[None, :]
    attn_probs = jax.nn.softmax(jnp.where(causal, scores, -1e30), axis=-1).astype(jnp.bfloat16)
    return jnp.einsum("bhqk,bhke->bhqe", attn_probs, values, preferred_element_type=jnp.float32).astype(jnp.bfloat16)


def branch_partials(normed, cosine, sine, w_q, b_q, w_k, b_k, w_v, b_v, w_o, w_up, b_up, w_down):
    def project(weight, bias):
        return jnp.einsum("bld,dhe->bhle", normed, weight, preferred_element_type=jnp.float32) + bias.astype(jnp.float32)[None, :, None, :]

    q_rot = apply_rotary(project(w_q, b_q), cosine, sine).astype(jnp.bfloat16)
    k_rot = apply_rotary(project(w_k, b_k), cosine, sine).astype(jnp.bfloat16)
    values = project(w_v, b_v).astype(jnp.bfloat16)
    attended = causal_attention(q_rot, k_rot, values)
    up_act = jax.nn.gelu(jnp.einsum("bld,df->blf", normed, w_up, preferred_element_type=jnp.float32) + b_up.astype(jnp.float32), approximate=True).astype(jnp.bfloat16)
    return (jnp.einsum("bhle,hed->bld", attended, w_o, preferred_element_type=jnp.float32)
            + jnp.einsum("blf,fd->bld", up_act, w_down, preferred_element_type=jnp.float32))


def solution(mesh):
    tp_size = mesh.shape["tp"]
    head_spec = P(None, None, "tp", None)
    head_bias_spec = P(None, "tp", None)
    in_specs = (P("dp", "tp", None), P(), P(), head_spec, head_bias_spec, head_spec, head_bias_spec, head_spec, head_bias_spec,
                P(None, "tp", None, None), P(), P(None, None, "tp"), P(None, "tp"), P(None, "tp", None), P())

    def local_program(x_loc, ln_gain, ln_bias, w_q, b_q, w_k, b_k, w_v, b_v, w_o, b_o, w_up, b_up, w_down, b_down):
        cosine, sine = rotary_tables(x_loc.shape[1] * tp_size)
        hidden = x_loc
        for layer in range(w_q.shape[0]):
            normed = layer_norm(hidden, ln_gain[layer], ln_bias[layer])
            gathered = lax.all_gather(normed, "tp", axis=1, tiled=True)
            part_sum = branch_partials(gathered, cosine, sine, w_q[layer], b_q[layer], w_k[layer], b_k[layer], w_v[layer], b_v[layer],
                                       w_o[layer], w_up[layer], b_up[layer], w_down[layer]).astype(jnp.bfloat16)
            returned = lax.psum_scatter(part_sum, "tp", scatter_dimension=1, tiled=True)
            hidden = (hidden.astype(jnp.float32) + returned.astype(jnp.float32) + b_o[layer].astype(jnp.float32)
                      + b_down[layer].astype(jnp.float32)).astype(jnp.bfloat16)
        return hidden

    return jax.shard_map(local_program, mesh=mesh, in_specs=in_specs, out_specs=P("dp", "tp", None), check_vma=False)
```

profile of v0, /device:TPU:0, one launch (start us, length us, event | category | flops | bytes accessed | tf_op | source)
XLA Modules:
  0.0 817.1 jit_solution(980821020343709048)
XLA Ops:
  18.0 4.0 iota_compare_fusion
  22.1 6.3 fusion.137
  28.4 3.3 fusion.136
  33.8 51.8 %all-gather.3.cloned.1.call-done = bf16[1,2048,2560]{2,1,0:T(8,128)(2,1)} async-done(((bf16[1,512,2560]{2,1,0:T(8,128)(2,1)}), bf16[1,2048,2560]{2,1,0:T(8,128)(2,1)}) %all-gather.3.cloned.1.call-update) | async-done | bytes 10485776 | tf_op jit(solution)/shard_map/all_gather | solution.py:67
  85.6 10.9 %fusion.62 = f32[2048,640]{0,1:S(1)} fusion(bf16[2560,640]{0,1:T(8,128)(2,1)} %bitcast.190, bf16[1,2048,2560]{2,1,0:T(8,128)(2,1)} %all-gather.3.cloned.1.call-done), kind=kOutput, calls=%fused_computation.63 | convolution fusion | flops 6710886400 | bytes 19005440
  99.0 6.9 fusion.60
  109.7 50.2 %fusion.138 = f32[8,2048]{1,0:T(8,128)S(1)} fusion(pred[2048,2048]{0,1:T(8,128)(4,1)} %iota_compare_fusion, bf16[8,2048,48]{1,2,0:T(8,128)(2,1)} %fusion.107, bf16[8,2048,16]{1,2,0:T(8,128)(2,1)} %get-tuple-element.33, bf16[8,2048,16]{1,2,0:T(8,128)(2,1)} %get-tuple-element.34, bf16[8,2048,48]{1,2,0:T(8,128)(2,1)} %fusion.106, ...), kind=kOutput, calls=%fused_computation.174 | convolution fusion | flops 5518657536 | bytes 9502720 | tf_op jit(solution)/shard_map/sub | solution.py:38
  159.9 11.2 %fusion.58 = f32[2048,640]{0,1} fusion(bf16[2560,640]{0,1:T(8,128)(2,1)S(1)} %bitcast.188, bf16[1,2048,2560]{2,1,0:T(8,128)(2,1)} %all-gather.3.cloned.1.call-done), kind=kOutput, calls=%fused_computation.59 | convolution fusion | flops 6710886400 | bytes 19005440
  171.1 71.1 %fusion.97 = bf16[8,2048,80]{1,2,0:T(8,128)(2,1)} fusion(f32[8,2048]{1,0:T(8,128)S(1)} %fusion.138, pred[2048,2048]{0,1:T(8,128)(4,1)} %iota_compare_fusion, f32[8,80,1,2048]{3,1,0,2:T(8,128)} %bitcast.192, f32[8,80]{1,0:T(8,128)S(1)} %get-tuple-element.36, bf16[8,2048,48]{1,2,0:T(8,128)(2,1)} %fusion.107, bf16[8,2048,16]{1,2,0:T(8,128)(2,1)} %get-tuple-element.33, ...), kind=kOutput, calls=%fused_computation.104 | convolution fusion | flops 10924869632 | bytes 17369600 | tf_op jit(solution)/shard_map/bhqk,bhke->bhqe/dot_general | solution.py:39
  242.2 16.6 %fusion.90 = f32[2048,2560,1]{1,0,2:T(8,128)} fusion(bf16[8,2048,80]{1,2,0:T(8,128)(2,1)} %fusion.97, bf16[2,8,80,2560]{3,2,1,0:T(8,128)(2,1)} %param.24), kind=kOutput, calls=%fused_computation.99 | convolution fusion | flops 6710886400 | bytes 26869760 | tf_op jit(solution)/shard_map/bhle,hed->bld/dot_general | solution.py:51
  258.8 35.0 %fusion.19 = bf16[2048,2560]{1,0:T(8,128)(2,1)} fusion(bf16[2,2560,2560]{2,1,0:T(8,128)(2,1)S(1)} %copy-done.29, bf16[1,2048,2560]{2,1,0:T(8,128)(2,1)} %all-gather.3.cloned.1.call-done, f32[2560]{0:T(1024)S(1)} %copy-done.24), kind=kOutput, calls=%fused_computation.27 | convolution fusion | flops 26895974400 | bytes 34091008 | tf_op jit(solution)/shard_map/bld,df->blf/dot_general | solution.py:50
  293.8 35.8 %fusion.64 = bf16[1,2048,2560]{2,1,0:T(8,128)(2,1)} fusion(bf16[2048,2560]{1,0:T(8,128)(2,1)} %fusion.19, bf16[2,2560,2560]{2,1,0:T(8,128)(2,1)} %param.28, f32[2048,2560,1]{1,0,2:T(8,128)} %fusion.90), kind=kOutput, calls=%fused_computation.65 | convolution fusion | flops 26854031360 | bytes 55050240 | tf_op jit(solution)/shard_map/blf,fd->bld/dot_general | solution.py:52
  331.0 76.6 %reduce-scatter.3.cloned.1.call-done = bf16[1,512,2560]{2,1,0:T(8,128)(2,1)} async-done(((bf16[1,2048,2560]{2,1,0:T(8,128)(2,1)}), bf16[1,512,2560]{2,1,0:T(8,128)(2,1)}) %reduce-scatter.3.cloned.1.call-update) | async-done | bytes 2621456 | tf_op jit(solution)/shard_map/reduce_scatter | solution.py:70
  414.9 68.0 %all-gather.5.cloned.1.call-done = bf16[1,2048,2560]{2,1,0:T(8,128)(2,1)} async-done(((bf16[1,512,2560]{2,1,0:T(8,128)(2,1)}), bf16[1,2048,2560]{2,1,0:T(8,128)(2,1)}) %all-gather.5.cloned.1.call-update) | async-done | bytes 10485776 | tf_op jit(solution)/shard_map/all_gather | solution.py:67
  482.9 11.1 %fusion.55 = f32[2048,640]{0,1:S(1)} fusion(bf16[2560,640]{0,1:T(8,128)(2,1)S(1)} %bitcast.187, bf16[1,2048,2560]{2,1,0:T(8,128)(2,1)} %all-gather.5.cloned.1.call-done), kind=kOutput, calls=%fused_computation.56 | convolution fusion | flops 6710886400 | bytes 19005440
  496.5 7.0 fusion.53
  507.8 50.7 %fusion.139 = f32[8,2048]{1,0:T(8,128)S(1)} fusion(pred[2048,2048]{0,1:T(8,128)(4,1)} %iota_compare_fusion, bf16[8,2048,48]{1,2,0:T(8,128)(2,1)} %fusion.109, bf16[8,2048,16]{1,2,0:T(8,128)(2,1)} %get-tuple-element.31, bf16[8,2048,16]{1,2,0:T(8,128)(2,1)} %get-tuple-element.32, bf16[8,2048,48]{1,2,0:T(8,128)(2,1)} %fusion.108, ...), kind=kOutput, calls=%fused_computation.175 | convolution fusion | flops 5518657536 | bytes 9502720 | tf_op jit(solution)/shard_map/sub | solution.py:38
  558.5 11.2 %fusion.51 = f32[2048,640]{0,1} fusion(bf16[2560,640]{0,1:T(8,128)(2,1)S(1)} %bitcast.185, bf16[1,2048,2560]{2,1,0:T(8,128)(2,1)} %all-gather.5.cloned.1.call-done), kind=kOutput, calls=%fused_computation.52 | convolution fusion | flops 6710886400 | bytes 19005440
  569.7 70.9 %fusion.94 = bf16[8,2048,80]{1,2,0:T(8,128)(2,1)} fusion(f32[8,2048]{1,0:T(8,128)S(1)} %fusion.139, pred[2048,2048]{0,1:T(8,128)(4,1)} %iota_compare_fusion, f32[8,80,1,2048]{3,1,0,2:T(8,128)} %bitcast.191, f32[8,80]{1,0:T(8,128)S(1)} %copy-done.28, bf16[8,2048,48]{1,2,0:T(8,128)(2,1)} %fusion.109, bf16[8,2048,16]{1,2,0:T(8,128)(2,1)} %get-tuple-element.31, ...), kind=kOutput, calls=%fused_computation.103 | convolution fusion | flops 10924869632 | bytes 17369600 | tf_op jit(solution)/shard_map/bhqk,bhke->bhqe/dot_general | solution.py:39
  640.6 16.6 %fusion.88 = f32[2048,2560,1]{1,0,2:T(8,128)} fusion(bf16[8,2048,80]{1,2,0:T(8,128)(2,1)} %fusion.94, bf16[2,8,80,2560]{3,2,1,0:T(8,128)(2,1)} %param.24), kind=kOutput, calls=%fused_computation.97 | convolution fusion | flops 6710886400 | bytes 26869760 | tf_op jit(solution)/shard_map/bhle,hed->bld/dot_general | solution.py:51
  657.3 35.0 %fusion.27 = bf16[2048,2560]{1,0:T(8,128)(2,1)} fusion(bf16[2,2560,2560]{2,1,0:T(8,128)(2,1)S(1)} %copy-done.30, bf16[1,2048,2560]{2,1,0:T(8,128)(2,1)} %all-gather.5.cloned.1.call-done, f32[2560]{0:T(1024)S(1)} %copy-done.23), kind=kOutput, calls=%fused_computation.35 | convolution fusion | flops 26895974400 | bytes 34091008 | tf_op jit(solution)/shard_map/bld,df->blf/dot_general | solution.py:50
  692.3 35.9 %fusion.67 = bf16[1,2048,2560]{2,1,0:T(8,128)(2,1)} fusion(bf16[2048,2560]{1,0:T(8,128)(2,1)} %fusion.27, bf16[2,2560,2560]{2,1,0:T(8,128)(2,1)} %param.28, f32[2048,2560,1]{1,0,2:T(8,128)} %fusion.88), kind=kOutput, calls=%fused_computation.66 | convolution fusion | flops 26854031360 | bytes 55050240 | tf_op jit(solution)/shard_map/blf,fd->bld/dot_general | solution.py:52
  728.2 78.0 %reduce-scatter.5.cloned.1.call-done = bf16[1,512,2560]{2,1,0:T(8,128)(2,1)} async-done(((bf16[1,2048,2560]{2,1,0:T(8,128)(2,1)}), bf16[1,512,2560]{2,1,0:T(8,128)(2,1)}) %reduce-scatter.5.cloned.1.call-update) | async-done | bytes 2621456 | tf_op jit(solution)/shard_map/reduce_scatter | solution.py:70
  806.2 4.2 fusion.87
  (113 shorter events, 35.1 us)
Async XLA Ops:
  6.5 79.1 %all-gather.3.cloned.1.call-start = ((), (), s32[]{:S(2)}) async-start(), calls=%async_computation.2 | async-start | bytes 13107200 | tf_op jit(solution)/shard_map/all_gather | solution.py:67
  8.9 8.0 copy-start.27
  14.8 392.9 %reduce-scatter.3.cloned.1.call-start = ((), (), s32[]{:S(2)}) async-start(), calls=%async_computation.3 | async-start | bytes 13107200 | tf_op jit(solution)/shard_map/reduce_scatter | solution.py:70
  18.0 89.8 %copy-start.8 = (f32[2048,16]{0,1:T(8,128)}, f32[2048,16]{0,1:T(8,128)S(1)}, u32[]{:S(2)}) copy-start(f32[2048,16]{0,1:T(8,128)S(1)} %get-tuple-element.41) | copy-start | bytes 393220
  18.0 89.8 %copy-start.10 = (f32[2048,16]{0,1:T(8,128)}, f32[2048,16]{0,1:T(8,128)S(1)}, u32[]{:S(2)}) copy-start(f32[2048,16]{0,1:T(8,128)S(1)} %get-tuple-element.42) | copy-start | bytes 393220
  18.0 10.4 %slice-start = ((s8[6553600]{0:T(1024)(128)(4,1)}), s8[4194304]{0:T(1024)(128)(4,1)S(1)}, s32[]{:S(2)}) async-start(s8[6553600]{0:T(1024)(128)(4,1)} %bitcast.177), calls=%async_computation.6 | async-start | bytes 8388608
  18.0 13.7 %slice-start.2 = ((s8[6553600]{0:T(1024)(128)(4,1)}), s8[4194304]{0:T(1024)(128)(4,1)S(1)}, s32[]{:S(2)}) async-start(s8[6553600]{0:T(1024)(128)(4,1)} %bitcast.179), calls=%async_computation.8 | async-start | bytes 8388608
  22.1 9.6 %slice-start.3 = ((s8[6553600]{0:T(1024)(128)(4,1)}), s8[2359296]{0:T(1024)(128)(4,1)S(1)}, s32[]{:S(2)}) async-start(s8[6553600]{0:T(1024)(128)(4,1)} %bitcast.179), calls=%async_computation.9 | async-start | bytes 4718592
  85.6 12.7 %copy-start.31 = (bf16[1,2048,2560]{2,1,0:T(8,128)(2,1)S(1)}, bf16[1,2048,2560]{2,1,0:T(8,128)(2,1)}, u32[]{:S(2)}) copy-start(bf16[1,2048,2560]{2,1,0:T(8,128)(2,1)} %all-gather.3.cloned.1.call-done) | copy-start | bytes 31457284
  242.2 16.7 %copy-start.24 = (f32[2560]{0:T(1024)S(1)}, f32[2560]{0:T(1024)}, u32[]{:S(2)}) copy-start(f32[2560]{0:T(1024)} %get-tuple-element.10) | copy-start | bytes 30724
  242.2 16.7 %copy-start.29 = (bf16[2,2560,2560]{2,1,0:T(8,128)(2,1)S(1)}, bf16[2,2560,2560]{2,1,0:T(8,128)(2,1)}, u32[]{:S(2)}) copy-start(bf16[2,2560,2560]{2,1,0:T(8,128)(2,1)} %param.26) | copy-start | bytes 78643200
  329.6 78.0 %copy-start.1 = (bf16[1,512,2560]{2,1,0:T(8,128)(2,1)S(1)}, bf16[1,512,2560]{2,1,0:T(8,128)(2,1)}, u32[]{:S(2)}) copy-start(bf16[1,512,2560]{2,1,0:T(8,128)(2,1)} %param.15) | copy-start | bytes 7864324
  329.6 153.2 %all-gather.5.cloned.1.call-start = ((), (), s32[]{:S(2)}) async-start(), calls=%async_computation.4 | async-start | bytes 13107200 | tf_op jit(solution)/shard_map/all_gather | solution.py:67
  410.8 72.1 %copy-start.6 = (bf16[1,2560,8,80]{1,3,2,0:T(8,128)(2,1)S(1)}, bf16[1,2560,8,80]{1,3,2,0:T(8,128)(2,1)}, u32[]{:S(2)}) copy-start(bf16[1,2560,8,80]{1,3,2,0:T(8,128)(2,1)} %get-tuple-element.19) | copy-start | bytes 9830404
  414.8 391.3 %reduce-scatter.5.cloned.1.call-start = ((), (), s32[]{:S(2)}) async-start(), calls=%async_computation.5 | async-start | bytes 13107200 | tf_op jit(solution)/shard_map/reduce_scatter | solution.py:70
  482.9 11.2 %copy-start.22 = (f32[8,80]{1,0:T(8,128)S(1)}, f32[8,80]{1,0:T(8,128)}, u32[]{:S(2)}) copy-start(f32[8,80]{1,0:T(8,128)} %get-tuple-element.37) | copy-start | bytes 7684
  482.9 13.0 %copy-start.32 = (bf16[1,2048,2560]{2,1,0:T(8,128)(2,1)S(1)}, bf16[1,2048,2560]{2,1,0:T(8,128)(2,1)}, u32[]{:S(2)}) copy-start(bf16[1,2048,2560]{2,1,0:T(8,128)(2,1)} %all-gather.5.cloned.1.call-done) | copy-start | bytes 31457284
  507.8 50.7 %copy-start.4 = (bf16[1,2560,8,80]{1,3,2,0:T(8,128)(2,1)S(1)}, bf16[1,2560,8,80]{1,3,2,0:T(8,128)(2,1)}, u32[]{:S(2)}) copy-start(bf16[1,2560,8,80]{1,3,2,0:T(8,128)(2,1)} %get-tuple-element.17) | copy-start | bytes 9830404
  558.5 11.2 %copy-start.28 = (f32[8,80]{1,0:T(8,128)S(1)}, f32[8,80]{1,0:T(8,128)}, u32[]{:S(2)}) copy-start(f32[8,80]{1,0:T(8,128)} %get-tuple-element.35) | copy-start | bytes 7684
  640.6 16.6 %copy-start.23 = (f32[2560]{0:T(1024)S(1)}, f32[2560]{0:T(1024)}, u32[]{:S(2)}) copy-start(f32[2560]{0:T(1024)} %get-tuple-element.9) | copy-start | bytes 30724
  640.6 16.6 %copy-start.30 = (bf16[2,2560,2560]{2,1,0:T(8,128)(2,1)S(1)}, bf16[2,2560,2560]{2,1,0:T(8,128)(2,1)}, u32[]{:S(2)}) copy-start(bf16[2,2560,2560]{2,1,0:T(8,128)(2,1)} %param.26) | copy-start | bytes 78643200
  728.1 78.0 %copy-start.3 = (bf16[1,512,2560]{2,1,0:T(8,128)(2,1)S(1)}, bf16[1,512,2560]{2,1,0:T(8,128)(2,1)}, u32[]{:S(2)}) copy-start(bf16[1,512,2560]{2,1,0:T(8,128)(2,1)} %copy-done.2) | copy-start | bytes 7864324
  728.1 78.0 %copy-start.12 = (f32[2560]{0:T(1024)S(1)}, f32[2560]{0:T(1024)}, u32[]{:S(2)}) copy-start(f32[2560]{0:T(1024)} %get-tuple-element.7) | copy-start | bytes 30724
  728.1 78.0 %copy-start.13 = (f32[2560]{0:T(1024)S(1)}, f32[2560]{0:T(1024)}, u32[]{:S(2)}) copy-start(f32[2560]{0:T(1024)} %get-tuple-element.46) | copy-start | bytes 30724
  (17 other events, 68.3 us)
Sparse Core Ops, SparseCore 0:
  14.9 70.6 all-gather.2
  329.7 77.8 reduce-scatter.2
  415.0 67.8 all-gather.4
  728.3 77.8 reduce-scatter.4
where the time goes:
time: 820 us; the launch traced here: 817 us
  matrix products  476 us (58%)
  waiting for transfers between devices  274 us (33%)
  other arithmetic  32 us (4%)
  local copies, waits for them, and re-layouts  20.5 us (2%)
  between operations  13.7 us (2%)
    reduce_scatter x2, waiting for transfers between devices, local_program(): returned = lax.psum_scatter(part_sum, 'tp', scatter_dimension=1, tiled=True)  155 us
    dot_general x2, matrix products, causal_attention(): jnp.einsum('bhqk,bhke->bhqe', attn_probs, values, preferred_element_type=...  142 us
    all_gather x2, waiting for transfers between devices, local_program(): gathered = lax.all_gather(normed, 'tp', axis=1, tiled=True)  120 us
    sub x2, matrix products, causal_attention(): jax.nn.softmax(jnp.where(causal, scores, -1e+30), axis=-1)  101 us
    dot_general x2, matrix products, branch_partials(): jnp.einsum('blf,fd->bld', up_act, w_down, preferred_element_type=jnp.floa...  71.6 us
    dot_general x2, matrix products, branch_partials(): jnp.einsum('bld,df->blf', normed, w_up, preferred_element_type=jnp.float32)  70 us
    unnamed x6, matrix products  58.4 us
    dot_general x2, matrix products, branch_partials(): jnp.einsum('bhle,hed->bld', attended, w_o, preferred_element_type=jnp.flo...  33.3 us
  transfers between devices with their start and end apart: 4, of which 4 were waited for; matrix products, arithmetic and copies ran while one was open for 2% of the time, Pallas kernels for 0%

commit v1 on v0

v1 whole, which is shorter than its diff:
```python
import functools

import jax
import jax.numpy as jnp
import numpy as np
from jax import lax
from jax.experimental import pallas as pl
from jax.experimental.pallas import tpu as pltpu
from jax.sharding import PartitionSpec as P


F32, BF16 = jnp.float32, jnp.bfloat16
ROT_DIM = 32
UNIT = ROT_DIM // 2
ROPE_BASE = 10000.0
LN_EPS = 1e-5
LANES = 128
VMEM_LIMIT = 60 * 2**20
ROWS = 512
HEADS = 8
HEAD_DIM = 80
PAIRS = HEADS // 2
ANY = pl.BlockSpec(memory_space=pl.ANY)
VM = pl.BlockSpec(memory_space=pltpu.VMEM)


def packed_units():
    cols = [[None] * 8 for _ in range(5)]
    rest = []
    for p in range(PAIRS):
        base = 2 * (p % 2)
        for e in range(2):
            head = 2 * p + e
            cols[p][base + e] = (head, 0)
            cols[p + 1][base + e] = (head, 1)
    in_first = (6, 4, 2, 0)
    for p in range(PAIRS):
        units = [(2 * p + e, 2 + i) for e in range(2) for i in range(3)]
        rest.append((p, units[:in_first[p]], units[in_first[p]:]))
    for p, first, second in rest:
        for col, units in ((p, first), (p + 1, second)):
            for u in units:
                cols[col][cols[col].index(None)] = u
    return [u for col in cols for u in col]


UNITS = packed_units()
UNIT_ROWS = [h * HEAD_DIM + u * UNIT for h, u in UNITS]


def unit_runs():
    runs, start = [], 0
    for i in range(1, len(UNIT_ROWS) + 1):
        if i == len(UNIT_ROWS) or UNIT_ROWS[i] != UNIT_ROWS[i - 1] + UNIT:
            runs.append((UNIT_ROWS[start], start * UNIT, (i - start) * UNIT))
            start = i
    return runs


def head_masks():
    qk = np.zeros((HEADS, 1, 2 * LANES), np.float32)
    ov = np.zeros((HEADS, 1, 2 * LANES), np.float32)
    for i, (h, _) in enumerate(UNITS):
        lane = i * UNIT - (h // 2) * LANES
        qk[h, 0, lane:lane + UNIT] = 1.0
    for h in range(HEADS):
        lane = h * HEAD_DIM - (h // 2) * LANES
        ov[h, 0, lane:lane + HEAD_DIM] = 1.0
    return qk, ov


def gelu(x):
    return 0.5 * x * (1.0 + jnp.tanh(0.7978845608028654 * (x + 0.044715 * (x * x * x))))


def pre_kernel(nf, layer, n_pair, n_after, info, *refs):
    x_hbm, refs = refs[:2 * n_pair], refs[2 * n_pair:]
    (wq, wk, wv, bqkv_ref, cos_hbm, sin_hbm, wu, bu_ref, wd), refs = refs[:9], refs[9 + n_after:]
    q_out, k_out, v_out, mlp_out = refs[:4]
    x_s, tab_s, y_s, h_s, z_s, u_s, o_s, wp_s, wt_s, x_sem, p_sem, t_sem, h_sem, o_sem = refs[4:]
    R, _ = x_s.shape
    half = ROWS // 2
    nr = R // ROWS
    bf = wt_s.shape[2]
    N = HEADS * HEAD_DIM
    block, core = info[0], info[1]
    row0 = pl.multiple_of(core * half, half)
    row1 = pl.multiple_of((1 - core) * half, half)
    brow = pl.multiple_of(block * ROWS, ROWS)
    xcopies = []
    for p in range(n_pair):
        for s, row in enumerate((row0, row1)):
            xcopies.append(pltpu.make_async_copy(x_hbm[2 * p + s], x_s.at[pl.ds(p * ROWS + row, half)], x_sem.at[2 * p + s]))
    tcopies = [pltpu.make_async_copy(t.at[pl.ds(brow, R)], tab_s.at[s], x_sem.at[2 * n_pair + s]) for s, t in enumerate((cos_hbm, sin_hbm))]
    pcopies = []
    for s, w in enumerate((wq, wk)):
        for src, dst, n in unit_runs():
            pcopies.append(pltpu.make_async_copy(w.at[layer, pl.ds(src, n)], wp_s.at[pl.ds(s * N + dst, n)], p_sem.at[s]))
    pcopies.append(pltpu.make_async_copy(wv.at[layer], wp_s.at[pl.ds(2 * N, N)], p_sem.at[2]))
    pwaits = [pltpu.make_async_copy(w.at[layer], wp_s.at[pl.ds(s * N, N)], p_sem.at[s]) for s, w in enumerate((wq, wk, wv))]
    kv_rows = pl.ds(brow, R)
    hcopies = [pltpu.make_async_copy(h_s.at[0], q_out, h_sem.at[0]),
               pltpu.make_async_copy(h_s.at[1], k_out.at[kv_rows], h_sem.at[1]),
               pltpu.make_async_copy(h_s.at[2], v_out.at[kv_rows], h_sem.at[2])]

    def tile_copy(w, t, slot):
        return pltpu.make_async_copy(w.at[layer, :, pl.ds(pl.multiple_of(t * bf, bf), bf)], wt_s.at[slot], t_sem.at[slot])

    def out_copy(t):
        slot = lax.rem(t, 2)
        return pltpu.make_async_copy(o_s.at[slot], mlp_out.at[:, pl.ds(pl.multiple_of(t * bf, bf), bf)], o_sem.at[slot])

    def epilogue(r):
        step = 64
        lane = lax.broadcasted_iota(jnp.int32, (step, LANES), 1)
        low, mid = lane < 2 * UNIT, lane < 4 * UNIT
        high = jnp.logical_and(mid, jnp.logical_not(low))
        for rr in range(r * ROWS, (r + 1) * ROWS, step):
            rows = slice(rr, rr + step)
            cos, sin = tab_s[0, rows, :], tab_s[1, rows, :]
            cos_a, cos_ab, cos_b = jnp.where(low, cos, 1.0), jnp.where(mid, cos, 1.0), jnp.where(high, cos, 1.0)
            sin_a, sin_b = jnp.where(low, sin, 0.0), jnp.where(high, sin, 0.0)
            for s in range(3):
                c = [y_s[rows, s * N + i * LANES:s * N + (i + 1) * LANES] + bqkv_ref[:, s * N + i * LANES:s * N + (i + 1) * LANES] for i in range(5)]
                if s < 2:
                    c = [c[0] * cos_a - c[1] * sin_a,
                         c[1] * cos_ab + c[0] * sin_a - c[2] * sin_b,
                         c[2] * cos_ab + c[1] * sin_b - c[3] * sin_a,
                         c[3] * cos_ab + c[2] * sin_a - c[4] * sin_b,
                         c[4] * cos_b + c[3] * sin_b]
                for i in range(5):
                    h_s[s, rows, i * LANES:(i + 1) * LANES] = c[i].astype(BF16)

    def activate(t):
        step = 64
        slot = lax.rem(t, 2)
        bias = bu_ref[t].astype(F32)
        for rr in range(0, R, step):
            u_s[t + 1, rr:rr + step, :] = gelu(z_s[slot, rr:rr + step, :] + bias).astype(BF16)

    def slot3(t):
        return lax.rem(t, 3)

    for cp in xcopies:
        cp.start()
    tile_copy(wu, 0, 0).start()
    tile_copy(wu, 1, 1).start()
    for cp in pcopies + tcopies:
        cp.start()
    for cp in xcopies:
        cp.wait()

    def up_tile(t, first):
        tile_copy(wu, t, slot3(t)).wait()
        if isinstance(t, int):
            (tile_copy(wu, t + 2, slot3(t + 2)) if t + 2 < nf else tile_copy(wd, t + 2 - nf, slot3(t + 2))).start()
        else:
            @pl.when(t + 2 < nf)
            def _():
                tile_copy(wu, t + 2, slot3(t + 2)).start()

            @pl.when(t + 2 >= nf)
            def _():
                tile_copy(wd, t + 2 - nf, slot3(t + 2)).start()
        z_s[lax.rem(t, 2)] = jnp.dot(x_s[...], wt_s[slot3(t)], preferred_element_type=F32)
        if not first:
            activate(t - 1)

    if nr == 1:
        for t in range(nf):
            up_tile(t, t == 0)
    else:
        up_tile(0, True)
        lax.fori_loop(1, nf, lambda t, c: (up_tile(t, False), c)[1], 0)
    for cp in pwaits + tcopies:
        cp.wait()
    for r in range(nr):
        rows = slice(r * ROWS, (r + 1) * ROWS)
        y_s[rows, :] = lax.dot_general(x_s[rows, :], wp_s[...], (((1,), (1,)), ((), ())), preferred_element_type=F32)
        if r == 0:
            activate(nf - 1)
        else:
            epilogue(r - 1)

    def down_tile(t, first):
        slot = slot3(t + nf)
        tile_copy(wd, t, slot).wait()
        if isinstance(t, int):
            if t + 2 < nf:
                tile_copy(wd, t + 2, slot3(t + nf + 2)).start()
            if t >= 2:
                out_copy(t - 2).wait()
        else:
            @pl.when(t + 2 < nf)
            def _():
                tile_copy(wd, t + 2, slot3(t + nf + 2)).start()

            @pl.when(t >= 2)
            def _():
                out_copy(t - 2).wait()
        u = jnp.concatenate([u_s[f + 1] for f in range(nf)], axis=1)
        o = jnp.dot(u, wt_s[slot], preferred_element_type=F32)
        if first:
            epilogue(nr - 1)
        o_s[lax.rem(t, 2)] = o.astype(BF16)
        out_copy(t).start()
        if first:
            for cp in hcopies:
                cp.start()

    if nr == 1:
        for t in range(nf):
            down_tile(t, t == 0)
    else:
        down_tile(0, True)
        lax.fori_loop(1, nf, lambda t, c: (down_tile(t, False), c)[1], 0)
    out_copy(nf - 2).wait()
    out_copy(nf - 1).wait()
    for cp in hcopies:
        cp.wait()


def pre(layer, info, xs, wq, wk, wv, b_qkv, cos_t, sin_t, w_up, b_up, w_down, kg, vg, after, L, bf=512):
    half, D = xs[0].shape
    n_pair = len(xs) // 2
    R = n_pair * 2 * half
    F = w_up.shape[2]
    nf = F // bf
    N = HEADS * HEAD_DIM
    after = list(after)
    chain = [] if kg is None else [kg, vg]
    n0 = 1 + len(xs) + 9 + len(after)
    return pl.pallas_call(
        functools.partial(pre_kernel, nf, layer, n_pair, len(after) + len(chain)),
        grid_spec=pltpu.PrefetchScalarGridSpec(
            num_scalar_prefetch=1, grid=(),
            in_specs=[ANY] * (len(xs) + 3) + [VM, ANY, ANY, ANY, VM, ANY] + [ANY] * (len(after) + len(chain)),
            out_specs=[ANY] * 4,
            scratch_shapes=[pltpu.VMEM((R, D), BF16), pltpu.VMEM((2, R, LANES), F32), pltpu.VMEM((R, 3 * N), F32),
                            pltpu.VMEM((3, R, N), BF16), pltpu.VMEM((2, R, bf), F32), pltpu.VMEM((nf + 1, R, bf), BF16),
                            pltpu.VMEM((2, R, bf), BF16), pltpu.VMEM((3 * N, D), BF16), pltpu.VMEM((3, D, bf), BF16),
                            pltpu.SemaphoreType.DMA((2 * n_pair + 2,)), pltpu.SemaphoreType.DMA((3,)), pltpu.SemaphoreType.DMA((3,)),
                            pltpu.SemaphoreType.DMA((3,)), pltpu.SemaphoreType.DMA((2,))]),
        out_shape=[jax.ShapeDtypeStruct((R, N), BF16)] + [jax.ShapeDtypeStruct((L, N), BF16)] * 2 + [jax.ShapeDtypeStruct((R, D), BF16)],
        input_output_aliases={} if kg is None else {n0: 1, n0 + 1: 2}, name="pre",
        compiler_params=pltpu.CompilerParams(vmem_limit_bytes=VMEM_LIMIT),
        cost_estimate=pl.CostEstimate(flops=4 * R * D * F + 6 * R * D * N, bytes_accessed=4 * D * F + 4 * R * D, transcendentals=R * F),
    )(info, *xs, wq, wk, wv, b_qkv, cos_t, sin_t, w_up, b_up, w_down, *after, *chain)


def attn_kernel(layer, bases, n_blocks, n_after, info, qm_ref, om_ref, k_hbm, v_hbm, wo_hbm, *refs):
    q_hbm, mlp_hbm, refs = refs[:n_blocks], refs[n_blocks:2 * n_blocks], refs[2 * n_blocks:]
    mine_out, part_out, q_s, k_s, v_s, o_s, m_s, w_s, r_s, in_sem, w_sem, out_sem = refs[n_after:]
    R = q_s.shape[0]
    half = ROWS // 2
    n_blk = R // half
    scale = (HEAD_DIM ** -0.5) * 1.4426950408889634
    cp_w = pltpu.make_async_copy(wo_hbm.at[layer], w_s, w_sem.at[0])
    cp_m = [pltpu.make_async_copy(m, m_s.at[pl.ds(i * ROWS, ROWS)], w_sem.at[1 + i]) for i, m in enumerate(mlp_hbm)]
    cp_in = [pltpu.make_async_copy(src, dst, in_sem.at[i]) for i, (src, dst) in enumerate(((k_hbm, k_s), (v_hbm, v_s)))]
    cp_in += [pltpu.make_async_copy(q, q_s.at[pl.ds(i * ROWS, ROWS)], in_sem.at[2 + i]) for i, q in enumerate(q_hbm)]
    for cp in cp_in:
        cp.start()
    cp_w.start()
    for cp in cp_m:
        cp.start()
    o_s[...] = jnp.zeros_like(o_s)
    for cp in cp_in:
        cp.wait()

    def run(base):
        def pair(p, carry):
            lanes = pl.ds(pl.multiple_of(p * LANES, LANES), 2 * LANES)
            tasks = [(e, i) for i in range(n_blk) for e in range(2)]

            def scores(e, i):
                n = base + (i + 1) * half
                q = q_s[i * half:(i + 1) * half, lanes] * qm_ref[2 * p + e]
                return lax.dot_general(q, k_s[:n, lanes], (((1,), (1,)), ((), ())), preferred_element_type=F32)

            def rest(s, e, i):
                n = base + (i + 1) * half
                row = lax.broadcasted_iota(jnp.int32, (half, half), 0)
                col = lax.broadcasted_iota(jnp.int32, (half, half), 1)
                diag = jnp.where(row >= col, s[:, n - half:], -1e30)
                s = jnp.concatenate([s[:, :n - half], diag], axis=1) if n > half else diag
                m = jnp.max(s, axis=1, keepdims=True)
                prob = jnp.exp2((s - m) * scale)
                den = jnp.sum(prob, axis=1, keepdims=True)
                o = jnp.dot(prob.astype(BF16), v_s[:n, lanes], preferred_element_type=F32)
                o = jnp.where(om_ref[2 * p + e] > 0.5, o * (1.0 / den), 0.0)
                rows = slice(i * half, (i + 1) * half)
                o_s[rows, lanes] = o_s[rows, lanes] + o.astype(BF16)

            s = scores(*tasks[0])
            for a, t in enumerate(tasks):
                nxt = scores(*tasks[a + 1]) if a + 1 < len(tasks) else None
                rest(s, *t)
                s = nxt
            return carry

        lax.fori_loop(0, PAIRS, pair, 0)

    @pl.when(info[0] < 2)
    def _():
        run(bases[0])

    @pl.when(info[0] >= 2)
    def _():
        run(bases[1])

    cp_w.wait()
    for cp in cp_m:
        cp.wait()
    core = info[1]
    copies = []
    for i in range(n_blk):
        rows = slice(i * half, (i + 1) * half)
        r_s[rows, :] = (jnp.dot(o_s[rows, :], w_s[...], preferred_element_type=F32) + m_s[rows, :].astype(F32)).astype(BF16)
        if i % 2 == 1:
            p = i // 2
            for s, (ref, hf) in enumerate(((mine_out, core), (part_out, 1 - core))):
                cp = pltpu.make_async_copy(r_s.at[pl.ds(pl.multiple_of(p * ROWS + hf * half, half), half)], ref.at[pl.ds(p * half, half)], out_sem.at[2 * p + s])
                cp.start()
                copies.append(cp)
    for cp in copies:
        cp.wait()


def attn(layer, bases, info, masks, q, kg, vg, mlp_part, w_o, after=()):
    n_blocks, N = len(q), q[0].shape[1]
    R = n_blocks * ROWS
    L = kg.shape[0]
    D = w_o.shape[2]
    after = list(after)
    return pl.pallas_call(
        functools.partial(attn_kernel, layer, bases, n_blocks, len(after)),
        grid_spec=pltpu.PrefetchScalarGridSpec(
            num_scalar_prefetch=1, grid=(),
            in_specs=[VM, VM] + [ANY] * (3 + 2 * n_blocks + len(after)),
            out_specs=[ANY, ANY],
            scratch_shapes=[pltpu.VMEM((R, N), BF16), pltpu.VMEM((L, N), BF16), pltpu.VMEM((L, N), BF16), pltpu.VMEM((R, N), BF16),
                            pltpu.VMEM((R, D), BF16), pltpu.VMEM((N, D), BF16), pltpu.VMEM((R, D), BF16),
                            pltpu.SemaphoreType.DMA((2 + n_blocks,)), pltpu.SemaphoreType.DMA((1 + n_blocks,)), pltpu.SemaphoreType.DMA((2 * n_blocks,))]),
        out_shape=[jax.ShapeDtypeStruct((R // 2, D), BF16)] * 2, name="attn",
        compiler_params=pltpu.CompilerParams(vmem_limit_bytes=VMEM_LIMIT),
        cost_estimate=pl.CostEstimate(flops=4 * HEADS * R * (L // 2) * 128 + 2 * R * D * N, bytes_accessed=4 * L * N, transcendentals=HEADS * R * L // 2),
    )(info, *masks, kg, vg, w_o, *q, *mlp_part, *after)


def rotary_tables(seq_len):
    inv_freq = 1.0 / (ROPE_BASE ** (jnp.arange(UNIT, dtype=F32) * (2.0 / ROT_DIM)))
    angles = jnp.arange(seq_len, dtype=F32)[:, None] * inv_freq[None, :]
    return jnp.tile(jnp.cos(angles), (1, LANES // UNIT)), jnp.tile(jnp.sin(angles), (1, LANES // UNIT))


def layer_norm(x_f32, gain, bias):
    mean = jnp.mean(x_f32, axis=-1, keepdims=True)
    centered = x_f32 - mean
    variance = jnp.mean(centered * centered, axis=-1, keepdims=True)
    return (centered * lax.rsqrt(variance + LN_EPS) * gain.astype(F32) + bias.astype(F32)).astype(BF16)


def solution(mesh):
    head_spec = P(None, None, "tp", None)
    head_bias_spec = P(None, "tp", None)
    in_specs = (P("dp", "tp", None), P(), P(), head_spec, head_bias_spec, head_spec, head_bias_spec, head_spec, head_bias_spec,
                P(None, "tp", None, None), P(), P(None, None, "tp"), P(None, "tp"), P(None, "tp", None), P())
    across = [(0, 2), (1, 3), (2, 0), (3, 1)]
    partner = [(0, 1), (1, 0), (2, 3), (3, 2)]

    def to_chip(a):
        return lax.ppermute(a, "tp", across)

    def to_core(a):
        return lax.ppermute(a, "tp", partner)

    def behind(a, done):
        return lax.optimization_barrier((a, done))[0]

    def local_program(x_loc, ln_gain, ln_bias, w_q, b_q, w_k, b_k, w_v, b_v, w_o, b_o, w_up, b_up, w_down, b_down):
        n_layers, d_model, heads, head_dim = w_q.shape
        width = heads * head_dim
        half = x_loc.shape[1] // 2
        seq_len = 4 * x_loc.shape[1]
        index = lax.axis_index("tp")
        chip, core = index // 2, index % 2
        cos_t, sin_t = rotary_tables(seq_len)
        qk_mask, out_mask = head_masks()
        masks = (jnp.asarray(qk_mask, BF16), jnp.asarray(out_mask, F32))
        w_o2 = w_o.reshape(n_layers, width, d_model)
        w_qt, w_kt, w_vt = (jnp.transpose(w, (0, 2, 3, 1)).reshape(n_layers, width, d_model) for w in (w_q, w_k, w_v))

        def pick(first, second):
            return jnp.where(core == 0, first, second)

        def packed(bias):
            flat = bias.astype(F32).reshape(width)
            return jnp.concatenate([flat[r:r + UNIT] for r in UNIT_ROWS])

        x_halves = x_loc[0, :half], x_loc[0, half:]
        keep = pick(*x_halves)
        recv = to_core(pick(x_halves[1], x_halves[0]))
        res = [pick(keep, recv), pick(recv, keep)]
        info_own = [jnp.stack([2 * chip + j, core]).astype(jnp.int32) for j in range(2)]
        info_oth = [jnp.stack([2 * (1 - chip) + j, core]).astype(jnp.int32) for j in range(2)]

        def run_layer(layer, res):
            b_qkv = jnp.concatenate([packed(b_q[layer]), packed(b_k[layer]), b_v[layer].astype(F32).reshape(width)])[None]
            b_up3 = b_up[layer].reshape(-1, 1, 512)
            norm = [layer_norm(res[j].astype(F32), ln_gain[layer], ln_bias[layer]) for j in range(2)]
            far = [None, None]
            for j in range(2):
                far[j] = to_chip(norm[j])
            near = [to_core(norm[j]) for j in range(2)]

            def project(info, a, b, kg, vg, after):
                return pre(layer, info, [a, b], w_qt, w_kt, w_vt, b_qkv, cos_t, sin_t, w_up, b_up3, w_down, kg, vg, after, seq_len)

            q_own, mlp_own, relay = [None, None], [None, None], [None, None]
            kg = vg = None
            after = []
            for j in range(2):
                q_own[j], kg, vg, mlp_own[j] = project(info_own[j], norm[j], near[j], kg, vg, after)
                far[j] = behind(far[j], mlp_own[j])
                relay[j] = to_core(far[j])
                after = [far[j]]
            arrived = [None, None]
            for j in range(2):
                q_oth, kg, vg, mlp_oth = project(info_oth[j], far[j], relay[j], kg, vg, after)
                mine, other = attn(layer, (j * ROWS, (j + 2) * ROWS), info_oth[j], masks, [q_oth], kg, vg, [mlp_oth], w_o2)
                summed = (mine.astype(F32) + to_core(other).astype(F32)).astype(BF16)
                arrived[j] = to_chip(summed)
                after = [summed]
            mine, other = attn(layer, (0, 2 * ROWS), info_own[0], masks, q_own, kg, vg, mlp_own, w_o2, after)
            own = mine.astype(F32) + to_core(other).astype(F32)
            return [(res[j].astype(F32) + own[j * half:(j + 1) * half] + arrived[j].astype(F32) + b_o[layer].astype(F32)
                     + b_down[layer].astype(F32)).astype(BF16) for j in range(2)]

        for layer in range(n_layers):
            res = run_layer(layer, res)

        recv = to_core(pick(res[1], res[0]))
        keep = pick(res[0], res[1])
        return jnp.stack([pick(keep, recv), pick(recv, keep)]).reshape(x_loc.shape)

    return jax.shard_map(local_program, mesh=mesh, in_specs=in_specs, out_specs=P("dp", "tp", None), check_vma=False)
```

time: 820 us -> 555 us (0.68)
  matrix products: 476 us -> 0 us
  Pallas kernels: 0 us -> 357 us
  waiting for transfers between devices: 274 us -> 126 us
  between operations: 13.7 us -> 0.68 us
  starting transfers between devices: 0.3 us -> 13.3 us
    pallas_call x0 -> x14, Pallas kernels: none -> 357 us  [the longest x8 232 us: pre(): pl.pallas_call(functools.partial(pre_kernel, nf, layer, n_pair, len(after...]
    dot_general x8 -> x0, matrix products: 317 us -> none  [the longest x2 142 us: causal_attention(): jnp.einsum('bhqk,bhke->bhqe', attn_probs, values, preferred_element_type=...]
    reduce_scatter x2 -> x0, waiting for transfers between devices: 155 us -> none  [local_program(): returned = lax.psum_scatter(part_sum, 'tp', scatter_dimension=1, tiled=True)]
    ppermute x0 -> x24, waiting for transfers between devices: none -> 126 us  [the longest x8 105 us: to_chip(): return lax.ppermute(a, 'tp', across)]
    all_gather x2 -> x0, waiting for transfers between devices: 120 us -> none  [local_program(): gathered = lax.all_gather(normed, 'tp', axis=1, tiled=True)]
    sub x2 -> x0, matrix products: 101 us -> none  [causal_attention(): jax.nn.softmax(jnp.where(causal, scores, -1e+30), axis=-1)]
    unnamed x6 -> x0, matrix products: 58.4 us -> none
    ppermute x0 -> x24, starting transfers between devices: none -> 13.3 us  [the longest x8 9.01 us: to_chip(): return lax.ppermute(a, 'tp', across)]
  transfers between devices with their start and end apart: 4 -> 24, of which waited for: 4 -> 14; matrix products, arithmetic and copies ran while one was open for 2% -> 4% of each run, Pallas kernels for 0% -> 21%
where the time goes in v1:
time: 555 us; the launch traced here: 545 us
  Pallas kernels  357 us (64%)
  waiting for transfers between devices  126 us (23%)
  other arithmetic  35.1 us (6%)
  starting transfers between devices  13.3 us (2%)
  local copies, waits for them, and re-layouts  12.8 us (2%)
    pallas_call x8, Pallas kernels, pre(): pl.pallas_call(functools.partial(pre_kernel, nf, layer, n_pair, len(after...  232 us
    pallas_call x6, Pallas kernels, attn(): pl.pallas_call(functools.partial(attn_kernel, layer, bases, n_blocks, len...  125 us
    ppermute x8, waiting for transfers between devices, to_chip(): return lax.ppermute(a, 'tp', across)  105 us
    ppermute x16, waiting for transfers between devices, to_core(): return lax.ppermute(a, 'tp', partner)  20.7 us
  transfers between devices with their start and end apart: 24, of which 14 were waited for; matrix products, arithmetic and copies ran while one was open for 4% of the time, Pallas kernels for 21%

profile of v1, /device:TPU:0, one launch (start us, length us, event | category | flops | bytes accessed | tf_op | source)
XLA Modules:
  0.0 544.6 jit_solution(8527976451857771928)
XLA Ops:
  0.0 3.1 select_bitcast_fusion.2
  7.0 2.8 convert_reduce_fusion.2
  25.0 28.8 %pre.8 = (bf16[512,640]{1,0:T(8,128)(2,1)}, bf16[2048,640]{1,0:T(8,128)(2,1)}, bf16[2048,640]{1,0:T(8,128)(2,1)}, bf16[512,2560]{1,0:T(8,128)(2,1)}) custom-call(s32[2]{0:T(128)} %get-tuple-element.248.info, bf16[256,2560]{1,0:T(8,128)(2,1)} %copy-done.7, bf16[256,2560]{1,0:T(8,128)(2,1)} %collective-permute-done.4.refs_1_, bf16[2,640,2560]{2,1,0:T(8,128)(2,1)} %bitcast.31, ...), custom_call_target="tpu_custom_call" | custom-call | flops 18454937600 | bytes 31457280 | tf_op jit(solution)/shard_map/pre/pallas_call | solution.py:233
  54.4 28.8 %pre.9 = (bf16[512,640]{1,0:T(8,128)(2,1)}, bf16[2048,640]{1,0:T(8,128)(2,1)}, bf16[2048,640]{1,0:T(8,128)(2,1)}, bf16[512,2560]{1,0:T(8,128)(2,1)}) custom-call(s32[2]{0:T(128)} %get-tuple-element.249.info, bf16[256,2560]{1,0:T(8,128)(2,1)} %copy-done.5, ...), custom_call_target="tpu_custom_call", output_to_operand_aliasing={{1}: (13, {}), {2}: (14, {})} | custom-call | flops 18454937600 | bytes 31457280 | tf_op jit(solution)/shard_map/pre/pallas_call | solution.py:233
  84.4 29.3 %pre.10 = (bf16[512,640]{1,0:T(8,128)(2,1)}, bf16[2048,640]{1,0:T(8,128)(2,1)}, bf16[2048,640]{1,0:T(8,128)(2,1)}, bf16[512,2560]{1,0:T(8,128)(2,1)}) custom-call(s32[2]{0:T(128)} %pad_add_fusion.3.info, bf16[256,2560]{1,0:T(8,128)(2,1)} %collective-permute-done.3.refs_11_.refs_0_, ...), custom_call_target="tpu_custom_call", output_to_operand_aliasing={{1}: (13, {}), {2}: (14, {})} | custom-call | flops 18454937600 | bytes 31457280 | tf_op jit(solution)/shard_map/pre/pallas_call | solution.py:233
  113.7 18.9 %attn.6 = (bf16[256,2560]{1,0:T(8,128)(2,1)}, bf16[256,2560]{1,0:T(8,128)(2,1)}) custom-call(s32[2]{0:T(128)} %pad_add_fusion.3.info, bf16[8,1,256]{2,1,0:T(2,128)(2,1)} %constant.53.clone.qm_ref, f32[8,1,256]{2,1,0:T(1,128)} %constant.54.clone.om_ref, bf16[2048,640]{1,0:T(8,128)(2,1)} %get-tuple-element.61.k_hbm.refs_12_, ...), custom_call_target="tpu_custom_call" | custom-call | flops 3825205248 | bytes 5242880 | tf_op jit(solution)/shard_map/attn/pallas_call | solution.py:336
  139.8 29.1 %pre.11 = (bf16[512,640]{1,0:T(8,128)(2,1)}, bf16[2048,640]{1,0:T(8,128)(2,1)}, bf16[2048,640]{1,0:T(8,128)(2,1)}, bf16[512,2560]{1,0:T(8,128)(2,1)}) custom-call(s32[2]{0:T(128)} %pad_add_fusion.1.info, bf16[256,2560]{1,0:T(8,128)(2,1)} %collective-permute-done.1.refs_11_.refs_0_, ...), custom_call_target="tpu_custom_call", output_to_operand_aliasing={{1}: (13, {}), {2}: (14, {})} | custom-call | flops 18454937600 | bytes 31457280 | tf_op jit(solution)/shard_map/pre/pallas_call | solution.py:233
  168.9 21.7 %attn.7 = (bf16[256,2560]{1,0:T(8,128)(2,1)}, bf16[256,2560]{1,0:T(8,128)(2,1)}) custom-call(s32[2]{0:T(128)} %pad_add_fusion.1.info, bf16[8,1,256]{2,1,0:T(2,128)(2,1)} %constant.53.clone.qm_ref, f32[8,1,256]{2,1,0:T(1,128)} %constant.54.clone.om_ref, bf16[2048,640]{1,0:T(8,128)(2,1)} %get-tuple-element.67.k_hbm, ...), custom_call_target="tpu_custom_call" | custom-call | flops 3825205248 | bytes 5242880 | tf_op jit(solution)/shard_map/attn/pallas_call | solution.py:336
  191.0 2.9 collective-permute-done.8
  196.7 21.9 %attn.8 = (bf16[512,2560]{1,0:T(8,128)(2,1)}, bf16[512,2560]{1,0:T(8,128)(2,1)}) custom-call(s32[2]{0:T(128)} %get-tuple-element.248.info, bf16[8,1,256]{2,1,0:T(2,128)(2,1)} %constant.53.clone.qm_ref, f32[8,1,256]{2,1,0:T(1,128)} %constant.54.clone.om_ref, bf16[2048,640]{1,0:T(8,128)(2,1)} %get-tuple-element.67.k_hbm, ...), custom_call_target="tpu_custom_call" | custom-call | flops 7650410496 | bytes 5242880 | tf_op jit(solution)/shard_map/attn/pallas_call | solution.py:336
  226.4 24.3 %collective-permute-done.10 = bf16[256,2560]{1,0:T(8,128)(2,1)S(1)} collective-permute-done((bf16[256,2560]{1,0:T(8,128)(2,1)S(1)}, bf16[256,2560]{1,0:T(8,128)(2,1)S(1)}, u32[]{:S(2)}, u32[]{:S(2)}) %collective-permute-start.10) | collective-permute-done | bytes 1310752 | tf_op jit(solution)/shard_map/ppermute | solution.py:373
  250.6 27.3 %collective-permute-done.11 = bf16[256,2560]{1,0:T(8,128)(2,1)S(1)} collective-permute-done((bf16[256,2560]{1,0:T(8,128)(2,1)S(1)}, bf16[256,2560]{1,0:T(8,128)(2,1)S(1)}, u32[]{:S(2)}, u32[]{:S(2)}) %collective-permute-start.11) | collective-permute-done | bytes 1310752 | tf_op jit(solution)/shard_map/ppermute | solution.py:373
  286.6 28.8 %pre.12 = (bf16[512,640]{1,0:T(8,128)(2,1)}, bf16[2048,640]{1,0:T(8,128)(2,1)}, bf16[2048,640]{1,0:T(8,128)(2,1)}, bf16[512,2560]{1,0:T(8,128)(2,1)}) custom-call(s32[2]{0:T(128)} %get-tuple-element.248.info, bf16[256,2560]{1,0:T(8,128)(2,1)} %get-tuple-element.127.refs_0_, bf16[256,2560]{1,0:T(8,128)(2,1)} %collective-permute-done.15.refs_1_, ...), custom_call_target="tpu_custom_call" | custom-call | flops 18454937600 | bytes 31457280 | tf_op jit(solution)/shard_map/pre/pallas_call | solution.py:233
  316.3 29.3 %pre.13 = (bf16[512,640]{1,0:T(8,128)(2,1)}, bf16[2048,640]{1,0:T(8,128)(2,1)}, bf16[2048,640]{1,0:T(8,128)(2,1)}, bf16[512,2560]{1,0:T(8,128)(2,1)}) custom-call(s32[2]{0:T(128)} %get-tuple-element.249.info, bf16[256,2560]{1,0:T(8,128)(2,1)} %get-tuple-element.126.refs_0_, ...), custom_call_target="tpu_custom_call", output_to_operand_aliasing={{1}: (13, {}), {2}: (14, {})} | custom-call | flops 18454937600 | bytes 31457280 | tf_op jit(solution)/shard_map/pre/pallas_call | solution.py:233
  345.6 29.1 %pre.14 = (bf16[512,640]{1,0:T(8,128)(2,1)}, bf16[2048,640]{1,0:T(8,128)(2,1)}, bf16[2048,640]{1,0:T(8,128)(2,1)}, bf16[512,2560]{1,0:T(8,128)(2,1)}) custom-call(s32[2]{0:T(128)} %pad_add_fusion.3.info, bf16[256,2560]{1,0:T(8,128)(2,1)} %collective-permute-done.14.refs_11_.refs_0_, ...), custom_call_target="tpu_custom_call", output_to_operand_aliasing={{1}: (13, {}), {2}: (14, {})} | custom-call | flops 18454937600 | bytes 31457280 | tf_op jit(solution)/shard_map/pre/pallas_call | solution.py:233
  374.8 18.9 %attn.9 = (bf16[256,2560]{1,0:T(8,128)(2,1)}, bf16[256,2560]{1,0:T(8,128)(2,1)}) custom-call(s32[2]{0:T(128)} %pad_add_fusion.3.info, bf16[8,1,256]{2,1,0:T(2,128)(2,1)} %constant.53.clone.qm_ref, f32[8,1,256]{2,1,0:T(1,128)} %constant.54.clone.om_ref, bf16[2048,640]{1,0:T(8,128)(2,1)} %get-tuple-element.85.k_hbm.refs_12_, ...), custom_call_target="tpu_custom_call" | custom-call | flops 3825205248 | bytes 5242880 | tf_op jit(solution)/shard_map/attn/pallas_call | solution.py:336
  394.2 2.8 collective-permute-done.18
  399.8 28.9 %pre.15 = (bf16[512,640]{1,0:T(8,128)(2,1)}, bf16[2048,640]{1,0:T(8,128)(2,1)}, bf16[2048,640]{1,0:T(8,128)(2,1)}, bf16[512,2560]{1,0:T(8,128)(2,1)}) custom-call(s32[2]{0:T(128)} %pad_add_fusion.1.info, bf16[256,2560]{1,0:T(8,128)(2,1)} %collective-permute-done.12.refs_11_.refs_0_, ...), custom_call_target="tpu_custom_call", output_to_operand_aliasing={{1}: (13, {}), {2}: (14, {})} | custom-call | flops 18454937600 | bytes 31457280 | tf_op jit(solution)/shard_map/pre/pallas_call | solution.py:233
  428.7 21.7 %attn.10 = (bf16[256,2560]{1,0:T(8,128)(2,1)}, bf16[256,2560]{1,0:T(8,128)(2,1)}) custom-call(s32[2]{0:T(128)} %pad_add_fusion.1.info, bf16[8,1,256]{2,1,0:T(2,128)(2,1)} %constant.53.clone.qm_ref, f32[8,1,256]{2,1,0:T(1,128)} %constant.54.clone.om_ref, bf16[2048,640]{1,0:T(8,128)(2,1)} %get-tuple-element.91.k_hbm, ...), custom_call_target="tpu_custom_call" | custom-call | flops 3825205248 | bytes 5242880 | tf_op jit(solution)/shard_map/attn/pallas_call | solution.py:336
  450.8 2.9 collective-permute-done.19
  456.5 22.0 %attn.11 = (bf16[512,2560]{1,0:T(8,128)(2,1)}, bf16[512,2560]{1,0:T(8,128)(2,1)}) custom-call(s32[2]{0:T(128)} %get-tuple-element.248.info, bf16[8,1,256]{2,1,0:T(2,128)(2,1)} %constant.53.clone.qm_ref, f32[8,1,256]{2,1,0:T(1,128)} %constant.54.clone.om_ref, bf16[2048,640]{1,0:T(8,128)(2,1)} %get-tuple-element.91.k_hbm, ...), custom_call_target="tpu_custom_call" | custom-call | flops 7650410496 | bytes 5242880 | tf_op jit(solution)/shard_map/attn/pallas_call | solution.py:336
  486.1 24.6 %collective-permute-done.21 = bf16[256,2560]{1,0:T(8,128)(2,1)S(1)} collective-permute-done((bf16[256,2560]{1,0:T(8,128)(2,1)}, bf16[256,2560]{1,0:T(8,128)(2,1)S(1)}, u32[]{:S(2)}, u32[]{:S(2)}) %collective-permute-start.21) | collective-permute-done | bytes 1310752 | tf_op jit(solution)/shard_map/ppermute | solution.py:373
  510.7 27.3 %collective-permute-done.22 = bf16[256,2560]{1,0:T(8,128)(2,1)S(1)} collective-permute-done((bf16[256,2560]{1,0:T(8,128)(2,1)}, bf16[256,2560]{1,0:T(8,128)(2,1)S(1)}, u32[]{:S(2)}, u32[]{:S(2)}) %collective-permute-start.22) | collective-permute-done | bytes 1310752 | tf_op jit(solution)/shard_map/ppermute | solution.py:373
  539.3 3.0 collective-permute-done.23
  (134 shorter events, 65.7 us)
Async XLA Ops:
  3.1 3.9 collective-permute-start
  11.9 13.1 %collective-permute-start.4 = (bf16[256,2560]{1,0:T(8,128)(2,1)S(1)}, bf16[256,2560]{1,0:T(8,128)(2,1)}, u32[]{:S(2)}, u32[]{:S(2)}) collective-permute-start(bf16[256,2560]{1,0:T(8,128)(2,1)S(1)} %get-tuple-element.129.refs_0_), channel_id=1, source_target_pairs={{0,1},{1,0},{2,3},{3,2},{4,5},{5,4},{6,7},{7,6}} | collective-permute-start | bytes 3932168 | tf_op jit(solution)/shard_map/ppermute | solution.py:376
  22.0 32.4 %collective-permute-start.3 = (bf16[256,2560]{1,0:T(8,128)(2,1)S(1)}, bf16[256,2560]{1,0:T(8,128)(2,1)}, u32[]{:S(2)}, u32[]{:S(2)}) collective-permute-start(bf16[256,2560]{1,0:T(8,128)(2,1)S(1)} %get-tuple-element.129.refs_0_), channel_id=1, source_target_pairs={{0,2},{1,3},{2,0},{3,1},{4,6},{5,7},{6,4},{7,5}} | collective-permute-start | bytes 3932168 | tf_op jit(solution)/shard_map/ppermute | solution.py:373
  24.6 29.7 %collective-permute-start.2 = (bf16[256,2560]{1,0:T(8,128)(2,1)S(1)}, bf16[256,2560]{1,0:T(8,128)(2,1)}, u32[]{:S(2)}, u32[]{:S(2)}) collective-permute-start(bf16[256,2560]{1,0:T(8,128)(2,1)S(1)} %get-tuple-element.128.refs_0_), channel_id=1, source_target_pairs={{0,1},{1,0},{2,3},{3,2},{4,5},{5,4},{6,7},{7,6}} | collective-permute-start | bytes 3932168 | tf_op jit(solution)/shard_map/ppermute | solution.py:376
  24.7 58.5 %collective-permute-start.1 = (bf16[256,2560]{1,0:T(8,128)(2,1)S(1)}, bf16[256,2560]{1,0:T(8,128)(2,1)}, u32[]{:S(2)}, u32[]{:S(2)}) collective-permute-start(bf16[256,2560]{1,0:T(8,128)(2,1)S(1)} %get-tuple-element.128.refs_0_), channel_id=1, source_target_pairs={{0,2},{1,3},{2,0},{3,1},{4,6},{5,7},{6,4},{7,5}} | collective-permute-start | bytes 3932168 | tf_op jit(solution)/shard_map/ppermute | solution.py:373
  54.4 28.9 %collective-permute-start.6 = (bf16[256,2560]{1,0:T(8,128)(2,1)}, bf16[256,2560]{1,0:T(8,128)(2,1)S(1)}, u32[]{:S(2)}, u32[]{:S(2)}) collective-permute-start(bf16[256,2560]{1,0:T(8,128)(2,1)} %collective-permute-done.3.refs_11_.refs_0_), channel_id=1, source_target_pairs={{0,1},{1,0},{2,3},{3,2},{4,5},{5,4},{6,7},{7,6}} | collective-permute-start | bytes 3932168 | tf_op jit(solution)/shard_map/ppermute | solution.py:376
  132.6 3.4 collective-permute-start.7
  133.2 5.6 %collective-permute-start.5 = (bf16[256,2560]{1,0:T(8,128)(2,1)}, bf16[256,2560]{1,0:T(8,128)(2,1)S(1)}, u32[]{:S(2)}, u32[]{:S(2)}) collective-permute-start(bf16[256,2560]{1,0:T(8,128)(2,1)} %collective-permute-done.1.refs_11_.refs_0_), channel_id=1, source_target_pairs={{0,1},{1,0},{2,3},{3,2},{4,5},{5,4},{6,7},{7,6}} | collective-permute-start | bytes 3932168 | tf_op jit(solution)/shard_map/ppermute | solution.py:376
  190.6 3.3 collective-permute-start.8
  218.6 5.1 collective-permute-start.9
  219.0 31.6 %collective-permute-start.10 = (bf16[256,2560]{1,0:T(8,128)(2,1)S(1)}, bf16[256,2560]{1,0:T(8,128)(2,1)S(1)}, u32[]{:S(2)}, u32[]{:S(2)}) collective-permute-start(bf16[256,2560]{1,0:T(8,128)(2,1)S(1)} %copy-done.6), channel_id=1, source_target_pairs={{0,2},{1,3},{2,0},{3,1},{4,6},{5,7},{6,4},{7,5}} | collective-permute-start | bytes 3932168 | tf_op jit(solution)/shard_map/ppermute | solution.py:373
  220.2 57.7 %collective-permute-start.11 = (bf16[256,2560]{1,0:T(8,128)(2,1)S(1)}, bf16[256,2560]{1,0:T(8,128)(2,1)S(1)}, u32[]{:S(2)}, u32[]{:S(2)}) collective-permute-start(bf16[256,2560]{1,0:T(8,128)(2,1)S(1)} %copy-done.8), channel_id=1, source_target_pairs={{0,2},{1,3},{2,0},{3,1},{4,6},{5,7},{6,4},{7,5}} | collective-permute-start | bytes 3932168 | tf_op jit(solution)/shard_map/ppermute | solution.py:373
  283.1 3.5 collective-permute-start.15
  284.4 32.0 %collective-permute-start.14 = (bf16[256,2560]{1,0:T(8,128)(2,1)}, bf16[256,2560]{1,0:T(8,128)(2,1)}, u32[]{:S(2)}, u32[]{:S(2)}) collective-permute-start(bf16[256,2560]{1,0:T(8,128)(2,1)} %get-tuple-element.127.refs_0_), channel_id=1, source_target_pairs={{0,2},{1,3},{2,0},{3,1},{4,6},{5,7},{6,4},{7,5}} | collective-permute-start | bytes 3932168 | tf_op jit(solution)/shard_map/ppermute | solution.py:373
  285.6 30.7 %collective-permute-start.13 = (bf16[256,2560]{1,0:T(8,128)(2,1)}, bf16[256,2560]{1,0:T(8,128)(2,1)}, u32[]{:S(2)}, u32[]{:S(2)}) collective-permute-start(bf16[256,2560]{1,0:T(8,128)(2,1)} %get-tuple-element.126.refs_0_), channel_id=1, source_target_pairs={{0,1},{1,0},{2,3},{3,2},{4,5},{5,4},{6,7},{7,6}} | collective-permute-start | bytes 3932168 | tf_op jit(solution)/shard_map/ppermute | solution.py:376
  285.8 59.8 %collective-permute-start.12 = (bf16[256,2560]{1,0:T(8,128)(2,1)}, bf16[256,2560]{1,0:T(8,128)(2,1)}, u32[]{:S(2)}, u32[]{:S(2)}) collective-permute-start(bf16[256,2560]{1,0:T(8,128)(2,1)} %get-tuple-element.126.refs_0_), channel_id=1, source_target_pairs={{0,2},{1,3},{2,0},{3,1},{4,6},{5,7},{6,4},{7,5}} | collective-permute-start | bytes 3932168 | tf_op jit(solution)/shard_map/ppermute | solution.py:373
  316.3 29.3 %collective-permute-start.17 = (bf16[256,2560]{1,0:T(8,128)(2,1)}, bf16[256,2560]{1,0:T(8,128)(2,1)}, u32[]{:S(2)}, u32[]{:S(2)}) collective-permute-start(bf16[256,2560]{1,0:T(8,128)(2,1)} %collective-permute-done.14.refs_11_.refs_0_), channel_id=1, source_target_pairs={{0,1},{1,0},{2,3},{3,2},{4,5},{5,4},{6,7},{7,6}} | collective-permute-start | bytes 3932168 | tf_op jit(solution)/shard_map/ppermute | solution.py:376
  393.6 3.4 collective-permute-start.18
  394.2 5.6 %collective-permute-start.16 = (bf16[256,2560]{1,0:T(8,128)(2,1)}, bf16[256,2560]{1,0:T(8,128)(2,1)}, u32[]{:S(2)}, u32[]{:S(2)}) collective-permute-start(bf16[256,2560]{1,0:T(8,128)(2,1)} %collective-permute-done.12.refs_11_.refs_0_), channel_id=1, source_target_pairs={{0,1},{1,0},{2,3},{3,2},{4,5},{5,4},{6,7},{7,6}} | collective-permute-start | bytes 3932168 | tf_op jit(solution)/shard_map/ppermute | solution.py:376
  450.4 3.3 collective-permute-start.19
  478.5 5.1 collective-permute-start.20
  478.8 31.9 %collective-permute-start.21 = (bf16[256,2560]{1,0:T(8,128)(2,1)}, bf16[256,2560]{1,0:T(8,128)(2,1)S(1)}, u32[]{:S(2)}, u32[]{:S(2)}) collective-permute-start(bf16[256,2560]{1,0:T(8,128)(2,1)} %add_convert_fusion.1.refs_11_), channel_id=1, source_target_pairs={{0,2},{1,3},{2,0},{3,1},{4,6},{5,7},{6,4},{7,5}} | collective-permute-start | bytes 3932168 | tf_op jit(solution)/shard_map/ppermute | solution.py:373
  479.4 58.6 %collective-permute-start.22 = (bf16[256,2560]{1,0:T(8,128)(2,1)}, bf16[256,2560]{1,0:T(8,128)(2,1)S(1)}, u32[]{:S(2)}, u32[]{:S(2)}) collective-permute-start(bf16[256,2560]{1,0:T(8,128)(2,1)} %add_convert_fusion.refs_4_), channel_id=1, source_target_pairs={{0,2},{1,3},{2,0},{3,1},{4,6},{5,7},{6,4},{7,5}} | collective-permute-start | bytes 3932168 | tf_op jit(solution)/shard_map/ppermute | solution.py:373
  539.3 3.1 collective-permute-start.23
  (19 other events, 269.1 us)

commit v2 on v1

--- a/solution.py
+++ b/solution.py
@@ -92,11 +92,9 @@
         for s, row in enumerate((row0, row1)):
             xcopies.append(pltpu.make_async_copy(x_hbm[2 * p + s], x_s.at[pl.ds(p * ROWS + row, half)], x_sem.at[2 * p + s]))
     tcopies = [pltpu.make_async_copy(t.at[pl.ds(brow, R)], tab_s.at[s], x_sem.at[2 * n_pair + s]) for s, t in enumerate((cos_hbm, sin_hbm))]
-    pcopies = []
-    for s, w in enumerate((wq, wk)):
-        for src, dst, n in unit_runs():
-            pcopies.append(pltpu.make_async_copy(w.at[layer, pl.ds(src, n)], wp_s.at[pl.ds(s * N + dst, n)], p_sem.at[s]))
-    pcopies.append(pltpu.make_async_copy(wv.at[layer], wp_s.at[pl.ds(2 * N, N)], p_sem.at[2]))
+    pcopies = [[pltpu.make_async_copy(w.at[layer, pl.ds(src, n)], wp_s.at[pl.ds(s * N + dst, n)], p_sem.at[s])
+                for src, dst, n in unit_runs()] for s, w in enumerate((wq, wk))]
+    pcopies.append([pltpu.make_async_copy(wv.at[layer], wp_s.at[pl.ds(2 * N, N)], p_sem.at[2])])
     pwaits = [pltpu.make_async_copy(w.at[layer], wp_s.at[pl.ds(s * N, N)], p_sem.at[s]) for s, w in enumerate((wq, wk, wv))]
     kv_rows = pl.ds(brow, R)
     hcopies = [pltpu.make_async_copy(h_s.at[0], q_out, h_sem.at[0]),
@@ -104,11 +102,11 @@
                pltpu.make_async_copy(h_s.at[2], v_out.at[kv_rows], h_sem.at[2])]
 
     def tile_copy(w, t, slot):
-        return pltpu.make_async_copy(w.at[layer, :, pl.ds(pl.multiple_of(t * bf, bf), bf)], wt_s.at[slot], t_sem.at[slot])
+        return pltpu.make_async_copy(w.at[layer, :, pl.ds(t * bf, bf)], wt_s.at[slot], t_sem.at[slot])
 
     def out_copy(t):
-        slot = lax.rem(t, 2)
-        return pltpu.make_async_copy(o_s.at[slot], mlp_out.at[:, pl.ds(pl.multiple_of(t * bf, bf), bf)], o_sem.at[slot])
+        slot = t % 2
+        return pltpu.make_async_copy(o_s.at[slot], mlp_out.at[:, pl.ds(t * bf, bf)], o_sem.at[slot])
 
     def epilogue(r):
         step = 64
@@ -133,45 +131,31 @@
 
     def activate(t):
         step = 64
-        slot = lax.rem(t, 2)
+        slot = t % 2
         bias = bu_ref[t].astype(F32)
         for rr in range(0, R, step):
             u_s[t + 1, rr:rr + step, :] = gelu(z_s[slot, rr:rr + step, :] + bias).astype(BF16)
 
     def slot3(t):
-        return lax.rem(t, 3)
+        return t % 3
 
     for cp in xcopies:
         cp.start()
     tile_copy(wu, 0, 0).start()
-    tile_copy(wu, 1, 1).start()
-    for cp in pcopies + tcopies:
-        cp.start()
     for cp in xcopies:
         cp.wait()
 
     def up_tile(t, first):
         tile_copy(wu, t, slot3(t)).wait()
-        if isinstance(t, int):
-            (tile_copy(wu, t + 2, slot3(t + 2)) if t + 2 < nf else tile_copy(wd, t + 2 - nf, slot3(t + 2))).start()
-        else:
-            @pl.when(t + 2 < nf)
-            def _():
-                tile_copy(wu, t + 2, slot3(t + 2)).start()
-
-            @pl.when(t + 2 >= nf)
-            def _():
-                tile_copy(wd, t + 2 - nf, slot3(t + 2)).start()
-        z_s[lax.rem(t, 2)] = jnp.dot(x_s[...], wt_s[slot3(t)], preferred_element_type=F32)
+        (tile_copy(wu, t + 1, slot3(t + 1)) if t + 1 < nf else tile_copy(wd, 0, slot3(nf))).start()
+        for cp in pcopies[t - 1] if 1 <= t <= 3 else tcopies if t == 0 else ():
+            cp.start()
+        z_s[t % 2] = jnp.dot(x_s[...], wt_s[slot3(t)], preferred_element_type=F32)
         if not first:
             activate(t - 1)
 
-    if nr == 1:
-        for t in range(nf):
-            up_tile(t, t == 0)
-    else:
-        up_tile(0, True)
-        lax.fori_loop(1, nf, lambda t, c: (up_tile(t, False), c)[1], 0)
+    for t in range(nf):
+        up_tile(t, t == 0)
     for cp in pwaits + tcopies:
         cp.wait()
     for r in range(nr):
@@ -185,35 +169,22 @@
     def down_tile(t, first):
         slot = slot3(t + nf)
         tile_copy(wd, t, slot).wait()
-        if isinstance(t, int):
-            if t + 2 < nf:
-                tile_copy(wd, t + 2, slot3(t + nf + 2)).start()
-            if t >= 2:
-                out_copy(t - 2).wait()
-        else:
-            @pl.when(t + 2 < nf)
-            def _():
-                tile_copy(wd, t + 2, slot3(t + nf + 2)).start()
-
-            @pl.when(t >= 2)
-            def _():
-                out_copy(t - 2).wait()
+        if t + 1 < nf:
+            tile_copy(wd, t + 1, slot3(t + nf + 1)).start()
+        if t >= 2:
+            out_copy(t - 2).wait()
         u = jnp.concatenate([u_s[f + 1] for f in range(nf)], axis=1)
         o = jnp.dot(u, wt_s[slot], preferred_element_type=F32)
         if first:
             epilogue(nr - 1)
-        o_s[lax.rem(t, 2)] = o.astype(BF16)
+        o_s[t % 2] = o.astype(BF16)
         out_copy(t).start()
         if first:
             for cp in hcopies:
                 cp.start()
 
-    if nr == 1:
-        for t in range(nf):
-            down_tile(t, t == 0)
-    else:
-        down_tile(0, True)
-        lax.fori_loop(1, nf, lambda t, c: (down_tile(t, False), c)[1], 0)
+    for t in range(nf):
+        down_tile(t, t == 0)
     out_copy(nf - 2).wait()
     out_copy(nf - 1).wait()
     for cp in hcopies:
@@ -248,27 +219,35 @@
     )(info, *xs, wq, wk, wv, b_qkv, cos_t, sin_t, w_up, b_up, w_down, *after, *chain)
 
 
-def attn_kernel(layer, bases, n_blocks, n_after, info, qm_ref, om_ref, k_hbm, v_hbm, wo_hbm, *refs):
+def attn_kernel(layer, bases, own, n_blocks, n_after, qm_ref, om_ref, k_hbm, v_hbm, wo_hbm, *refs):
     q_hbm, mlp_hbm, refs = refs[:n_blocks], refs[n_blocks:2 * n_blocks], refs[2 * n_blocks:]
-    mine_out, part_out, q_s, k_s, v_s, o_s, m_s, w_s, r_s, in_sem, w_sem, out_sem = refs[n_after:]
+    sum_out, q_s, k_s, v_s, o_s, m_s, w_s, tx_s, rx_s, r_s, in_sem, w_sem, out_sem, send_sem, recv_sem = refs[n_after:]
     R = q_s.shape[0]
     half = ROWS // 2
     n_blk = R // half
     scale = (HEAD_DIM ** -0.5) * 1.4426950408889634
+    index = lax.axis_index("tp")
+    chip, core = index // 2, lax.rem(index, 2)
+    partner = {"tp": 2 * chip + 1 - core}
+    barrier = pltpu.get_barrier_semaphore()
+    pl.semaphore_signal(barrier, inc=1, device_id=partner, device_id_type=pl.DeviceIdType.MESH)
     cp_w = pltpu.make_async_copy(wo_hbm.at[layer], w_s, w_sem.at[0])
     cp_m = [pltpu.make_async_copy(m, m_s.at[pl.ds(i * ROWS, ROWS)], w_sem.at[1 + i]) for i, m in enumerate(mlp_hbm)]
-    cp_in = [pltpu.make_async_copy(src, dst, in_sem.at[i]) for i, (src, dst) in enumerate(((k_hbm, k_s), (v_hbm, v_s)))]
-    cp_in += [pltpu.make_async_copy(q, q_s.at[pl.ds(i * ROWS, ROWS)], in_sem.at[2 + i]) for i, q in enumerate(q_hbm)]
-    for cp in cp_in:
-        cp.start()
-    cp_w.start()
-    for cp in cp_m:
-        cp.start()
-    o_s[...] = jnp.zeros_like(o_s)
-    for cp in cp_in:
-        cp.wait()
+    cp_q = [pltpu.make_async_copy(q, q_s.at[pl.ds(i * ROWS, ROWS)], in_sem.at[2 + i]) for i, q in enumerate(q_hbm)]
 
     def run(base):
+        seen = pl.ds(0, base + R)
+        cp_in = cp_q + [pltpu.make_async_copy(src.at[seen], dst.at[seen], in_sem.at[i])
+                        for i, (src, dst) in enumerate(((k_hbm, k_s), (v_hbm, v_s)))]
+        for cp in cp_in:
+            cp.start()
+        o_s[...] = jnp.zeros_like(o_s)
+        for cp in cp_in:
+            cp.wait()
+        cp_w.start()
+        for cp in cp_m:
+            cp.start()
+
         def pair(p, carry):
             lanes = pl.ds(pl.multiple_of(p * LANES, LANES), 2 * LANES)
             tasks = [(e, i) for i in range(n_blk) for e in range(2)]
@@ -301,57 +280,70 @@
 
         lax.fori_loop(0, PAIRS, pair, 0)
 
-    @pl.when(info[0] < 2)
+    @pl.when(chip == (0 if own else 1))
     def _():
         run(bases[0])
 
-    @pl.when(info[0] >= 2)
+    @pl.when(chip == (1 if own else 0))
     def _():
         run(bases[1])
 
     cp_w.wait()
     for cp in cp_m:
         cp.wait()
-    core = info[1]
-    copies = []
-    for i in range(n_blk):
-        rows = slice(i * half, (i + 1) * half)
-        r_s[rows, :] = (jnp.dot(o_s[rows, :], w_s[...], preferred_element_type=F32) + m_s[rows, :].astype(F32)).astype(BF16)
-        if i % 2 == 1:
-            p = i // 2
-            for s, (ref, hf) in enumerate(((mine_out, core), (part_out, 1 - core))):
-                cp = pltpu.make_async_copy(r_s.at[pl.ds(pl.multiple_of(p * ROWS + hf * half, half), half)], ref.at[pl.ds(p * half, half)], out_sem.at[2 * p + s])
-                cp.start()
-                copies.append(cp)
-    for cp in copies:
+    pl.semaphore_wait(barrier, 1)
+
+    def partial(block, which):
+        rows = pl.ds(pl.multiple_of(block * ROWS + which * half, half), half)
+        return jnp.dot(o_s[rows, :], w_s[...], preferred_element_type=F32) + m_s[rows, :].astype(F32)
+
+    sends = []
+    for b in range(n_blocks):
+        tx_s[b] = partial(b, 1 - core).astype(BF16)
+        cp = pltpu.make_async_remote_copy(src_ref=tx_s.at[b], dst_ref=rx_s.at[b], send_sem=send_sem.at[b], recv_sem=recv_sem.at[b],
+                                          device_id=partner, device_id_type=pl.DeviceIdType.MESH)
+        cp.start()
+        sends.append(cp)
+    outs = []
+    for b in range(n_blocks):
+        r_s[b] = partial(b, core)
+    for b in range(n_blocks):
+        sends[b].wait()
+        tx_s[b] = (r_s[b] + rx_s[b].astype(F32)).astype(BF16)
+        cp = pltpu.make_async_copy(tx_s.at[b], sum_out.at[pl.ds(b * half, half)], out_sem.at[b])
+        cp.start()
+        outs.append(cp)
+    for cp in outs:
         cp.wait()
 
 
-def attn(layer, bases, info, masks, q, kg, vg, mlp_part, w_o, after=()):
+def attn(layer, bases, own, call_id, masks, q, kg, vg, mlp_part, w_o, after=()):
     n_blocks, N = len(q), q[0].shape[1]
     R = n_blocks * ROWS
+    half = ROWS // 2
     L = kg.shape[0]
     D = w_o.shape[2]
     after = list(after)
+    dma = pltpu.SemaphoreType.DMA
     return pl.pallas_call(
-        functools.partial(attn_kernel, layer, bases, n_blocks, len(after)),
-        grid_spec=pltpu.PrefetchScalarGridSpec(
-            num_scalar_prefetch=1, grid=(),
-            in_specs=[VM, VM] + [ANY] * (3 + 2 * n_blocks + len(after)),
-            out_specs=[ANY, ANY],
-            scratch_shapes=[pltpu.VMEM((R, N), BF16), pltpu.VMEM((L, N), BF16), pltpu.VMEM((L, N), BF16), pltpu.VMEM((R, N), BF16),
-                            pltpu.VMEM((R, D), BF16), pltpu.VMEM((N, D), BF16), pltpu.VMEM((R, D), BF16),
-                            pltpu.SemaphoreType.DMA((2 + n_blocks,)), pltpu.SemaphoreType.DMA((1 + n_blocks,)), pltpu.SemaphoreType.DMA((2 * n_blocks,))]),
-        out_shape=[jax.ShapeDtypeStruct((R // 2, D), BF16)] * 2, name="attn",
-        compiler_params=pltpu.CompilerParams(vmem_limit_bytes=VMEM_LIMIT),
+        functools.partial(attn_kernel, layer, bases, own, n_blocks, len(after)),
+        in_specs=[VM, VM] + [ANY] * (3 + 2 * n_blocks + len(after)),
+        out_specs=ANY,
+        scratch_shapes=[pltpu.VMEM((R, N), BF16), pltpu.VMEM((L, N), BF16), pltpu.VMEM((L, N), BF16), pltpu.VMEM((R, N), BF16),
+                        pltpu.VMEM((R, D), BF16), pltpu.VMEM((N, D), BF16), pltpu.VMEM((n_blocks, half, D), BF16),
+                        pltpu.VMEM((n_blocks, half, D), BF16), pltpu.VMEM((n_blocks, half, D), F32),
+                        dma((2 + n_blocks,)), dma((1 + n_blocks,)), dma((n_blocks,)), dma((n_blocks,)), dma((n_blocks,))],
+        out_shape=jax.ShapeDtypeStruct((R // 2, D), BF16), name="attn",
+        compiler_params=pltpu.CompilerParams(vmem_limit_bytes=VMEM_LIMIT, collective_id=call_id, has_side_effects=True),
         cost_estimate=pl.CostEstimate(flops=4 * HEADS * R * (L // 2) * 128 + 2 * R * D * N, bytes_accessed=4 * L * N, transcendentals=HEADS * R * L // 2),
-    )(info, *masks, kg, vg, w_o, *q, *mlp_part, *after)
+    )(*masks, kg, vg, w_o, *q, *mlp_part, *after)
 
 
 def rotary_tables(seq_len):
-    inv_freq = 1.0 / (ROPE_BASE ** (jnp.arange(UNIT, dtype=F32) * (2.0 / ROT_DIM)))
+    unit = jnp.arange(LANES) % UNIT
+    inv_freq = 1.0 / (ROPE_BASE ** (unit.astype(F32) * (2.0 / ROT_DIM)))
     angles = jnp.arange(seq_len, dtype=F32)[:, None] * inv_freq[None, :]
-    return jnp.tile(jnp.cos(angles), (1, LANES // UNIT)), jnp.tile(jnp.sin(angles), (1, LANES // UNIT))
+    return jnp.cos(angles), jnp.sin(angles)
 
 
 def layer_norm(x_f32, gain, bias):
@@ -428,13 +420,11 @@
             arrived = [None, None]
             for j in range(2):
                 q_oth, kg, vg, mlp_oth = project(info_oth[j], far[j], relay[j], kg, vg, after)
-                mine, other = attn(layer, (j * ROWS, (j + 2) * ROWS), info_oth[j], masks, [q_oth], kg, vg, [mlp_oth], w_o2)
-                summed = (mine.astype(F32) + to_core(other).astype(F32)).astype(BF16)
+                summed = attn(layer, (j * ROWS, (j + 2) * ROWS), False, 3 * layer + j, masks, [q_oth], kg, vg, [mlp_oth], w_o2)
                 arrived[j] = to_chip(summed)
                 after = [summed]
-            mine, other = attn(layer, (0, 2 * ROWS), info_own[0], masks, q_own, kg, vg, mlp_own, w_o2, after)
-            own = mine.astype(F32) + to_core(other).astype(F32)
-            return [(res[j].astype(F32) + own[j * half:(j + 1) * half] + arrived[j].astype(F32) + b_o[layer].astype(F32)
+            own = attn(layer, (0, 2 * ROWS), True, 3 * layer + 2, masks, q_own, kg, vg, mlp_own, w_o2, after)
+            return [(res[j].astype(F32) + own[j * half:(j + 1) * half].astype(F32) + arrived[j].astype(F32) + b_o[layer].astype(F32)
                      + b_down[layer].astype(F32)).astype(BF16) for j in range(2)]
 
         for layer in range(n_layers):

time: 555 us -> 488 us (0.88)
  waiting for transfers between devices: 126 us -> 78.1 us
  local copies, waits for them, and re-layouts: 12.8 us -> 5.45 us
  other arithmetic: 35.1 us -> 28.9 us
    ppermute x8, waiting for transfers between devices: 105 us -> 74.2 us  [to_chip(): return lax.ppermute(a, 'tp', across)]
    ppermute x16 -> x10, waiting for transfers between devices: 20.7 us -> 3.97 us  [to_core(): return lax.ppermute(a, 'tp', partner)]
    convert_element_type x4 -> x0, other arithmetic: 11 us -> none  [run_layer(): summed = (mine.astype(F32) + to_core(other).astype(F32)).astype(BF16)]
    another operation x4 -> x0, local copies, waits for them, and re-layouts: 7.26 us -> none  [the longest x2 3.64 us: rotary_tables(): jnp.tile(jnp.cos(angles), (1, LANES // UNIT))]
  transfers between devices with their start and end apart: 24 -> 18, of which waited for: 14 -> 7; matrix products, arithmetic and copies ran while one was open for 4% -> 2% of each run, Pallas kernels for 21% -> 53%
where the time goes in v2:
time: 488 us; the launch traced here: 482 us
  Pallas kernels  357 us (73%)
  waiting for transfers between devices  78.1 us (16%)
  other arithmetic  28.9 us (6%)
  starting transfers between devices  11.6 us (2%)
  local copies, waits for them, and re-layouts  5.45 us (1%)
    pallas_call x8, Pallas kernels, pre(): pl.pallas_call(functools.partial(pre_kernel, nf, layer, n_pair, len(after...  236 us
    pallas_call x6, Pallas kernels, attn(): pl.pallas_call(functools.partial(attn_kernel, layer, bases, own, n_blocks...  121 us
    ppermute x8, waiting for transfers between devices, to_chip(): return lax.ppermute(a, 'tp', across)  74.2 us
  transfers between devices with their start and end apart: 18, of which 7 were waited for; matrix products, arithmetic and copies ran while one was open for 2% of the time, Pallas kernels for 53%

profile of v2, /device:TPU:0, one launch (start us, length us, event | category | flops | bytes accessed | tf_op | source)
XLA Modules:
  0.0 481.8 jit_solution(17784827591258441175)
XLA Ops:
  5.6 3.6 convert_reduce_fusion.2
  15.0 5.0 %fusion.40 = (f32[2048,128]{1,0:T(8,128)}, f32[2048,128]{1,0:T(8,128)}) fusion(f32[128]{0:T(128)S(1)} %fusion.45), kind=kLoop, calls=%fused_computation.62 | loop fusion | flops 262144 | bytes 2097664 | tf_op jit(solution)/shard_map/sin | solution.py:346
  20.7 2.6 collective-permute-start.3
  23.7 29.7 %pre.8 = (bf16[512,640]{1,0:T(8,128)(2,1)}, bf16[2048,640]{1,0:T(8,128)(2,1)}, bf16[2048,640]{1,0:T(8,128)(2,1)}, bf16[512,2560]{1,0:T(8,128)(2,1)}) custom-call(s32[2]{0:T(128)} %pad_add_fusion.2.info, bf16[256,2560]{1,0:T(8,128)(2,1)} %get-tuple-element.105.refs_0_, bf16[256,2560]{1,0:T(8,128)(2,1)} %collective-permute-done.4.refs_1_, ...), custom_call_target="tpu_custom_call" | custom-call | flops 18454937600 | bytes 31457280 | tf_op jit(solution)/shard_map/pre/pallas_call | solution.py:204
  53.6 29.4 %pre.9 = (bf16[512,640]{1,0:T(8,128)(2,1)}, bf16[2048,640]{1,0:T(8,128)(2,1)}, bf16[2048,640]{1,0:T(8,128)(2,1)}, bf16[512,2560]{1,0:T(8,128)(2,1)}) custom-call(s32[2]{0:T(128)} %pad_add_fusion.1.info, bf16[256,2560]{1,0:T(8,128)(2,1)} %get-tuple-element.104.refs_0_, ...), custom_call_target="tpu_custom_call", output_to_operand_aliasing={{1}: (13, {}), {2}: (14, {})} | custom-call | flops 18454937600 | bytes 31457280 | tf_op jit(solution)/shard_map/pre/pallas_call | solution.py:204
  83.4 29.4 %pre.10 = (bf16[512,640]{1,0:T(8,128)(2,1)}, bf16[2048,640]{1,0:T(8,128)(2,1)}, bf16[2048,640]{1,0:T(8,128)(2,1)}, bf16[512,2560]{1,0:T(8,128)(2,1)}) custom-call(s32[2]{0:T(128)} %pad_add_fusion.3.info, bf16[256,2560]{1,0:T(8,128)(2,1)} %collective-permute-done.3.refs_11_.refs_0_, ...), custom_call_target="tpu_custom_call", output_to_operand_aliasing={{1}: (13, {}), {2}: (14, {})} | custom-call | flops 18454937600 | bytes 31457280 | tf_op jit(solution)/shard_map/pre/pallas_call | solution.py:204
  112.8 18.9 %attn.6.refs_11_ = bf16[256,2560]{1,0:T(8,128)(2,1)} custom-call(bf16[8,1,256]{2,1,0:T(2,128)(2,1)} %constant.68.clone.qm_ref, f32[8,1,256]{2,1,0:T(1,128)} %constant.69.clone.om_ref, bf16[2048,640]{1,0:T(8,128)(2,1)} %get-tuple-element.49.k_hbm.refs_12_, bf16[2048,640]{1,0:T(8,128)(2,1)} %get-tuple-element.50.v_hbm.refs_13_, ...), custom_call_target="tpu_custom_call" | custom-call | flops 3825205248 | bytes 5242880 | tf_op jit(solution)/shard_map/attn/pallas_call | solution.py:328
  131.8 29.4 %pre.11 = (bf16[512,640]{1,0:T(8,128)(2,1)}, bf16[2048,640]{1,0:T(8,128)(2,1)}, bf16[2048,640]{1,0:T(8,128)(2,1)}, bf16[512,2560]{1,0:T(8,128)(2,1)}) custom-call(s32[2]{0:T(128)} %pad_add_fusion.info, bf16[256,2560]{1,0:T(8,128)(2,1)} %collective-permute-done.1.refs_11_.refs_0_, ...), custom_call_target="tpu_custom_call", output_to_operand_aliasing={{1}: (13, {}), {2}: (14, {})} | custom-call | flops 18454937600 | bytes 31457280 | tf_op jit(solution)/shard_map/pre/pallas_call | solution.py:204
  161.3 21.7 %attn.7.refs_4_ = bf16[256,2560]{1,0:T(8,128)(2,1)} custom-call(bf16[8,1,256]{2,1,0:T(2,128)(2,1)} %constant.68.clone.qm_ref, f32[8,1,256]{2,1,0:T(1,128)} %constant.69.clone.om_ref, bf16[2048,640]{1,0:T(8,128)(2,1)} %get-tuple-element.53.k_hbm, bf16[2048,640]{1,0:T(8,128)(2,1)} %get-tuple-element.54.v_hbm, bf16[2,640,2560]{2,1,0:T(8,128)(2,1)} %bitcast.54, ...), custom_call_target="tpu_custom_call" | custom-call | flops 3825205248 | bytes 5242880 | tf_op jit(solution)/shard_map/attn/pallas_call | solution.py:328
  185.2 20.0 %attn.8 = bf16[512,2560]{1,0:T(8,128)(2,1)} custom-call(bf16[8,1,256]{2,1,0:T(2,128)(2,1)} %constant.68.clone.qm_ref, f32[8,1,256]{2,1,0:T(1,128)} %constant.69.clone.om_ref, bf16[2048,640]{1,0:T(8,128)(2,1)} %get-tuple-element.53.k_hbm, bf16[2048,640]{1,0:T(8,128)(2,1)} %get-tuple-element.54.v_hbm, bf16[2,640,2560]{2,1,0:T(8,128)(2,1)} %bitcast.55, ...), custom_call_target="tpu_custom_call" | custom-call | flops 7650410496 | bytes 5242880 | tf_op jit(solution)/shard_map/attn/pallas_call | solution.py:328
  205.2 9.8 %collective-permute-done.8 = bf16[256,2560]{1,0:T(8,128)(2,1)} collective-permute-done((bf16[256,2560]{1,0:T(8,128)(2,1)}, bf16[256,2560]{1,0:T(8,128)(2,1)}, u32[]{:S(2)}, u32[]{:S(2)}) %collective-permute-start.8) | collective-permute-done | bytes 1310752 | tf_op jit(solution)/shard_map/ppermute | solution.py:365
  215.0 27.3 %collective-permute-done.7 = bf16[256,2560]{1,0:T(8,128)(2,1)} collective-permute-done((bf16[256,2560]{1,0:T(8,128)(2,1)}, bf16[256,2560]{1,0:T(8,128)(2,1)}, u32[]{:S(2)}, u32[]{:S(2)}) %collective-permute-start.7) | collective-permute-done | bytes 1310752 | tf_op jit(solution)/shard_map/ppermute | solution.py:365
  242.3 4.2 convert_reduce_fusion
  252.4 29.4 %pre.12 = (bf16[512,640]{1,0:T(8,128)(2,1)}, bf16[2048,640]{1,0:T(8,128)(2,1)}, bf16[2048,640]{1,0:T(8,128)(2,1)}, bf16[512,2560]{1,0:T(8,128)(2,1)}) custom-call(s32[2]{0:T(128)} %pad_add_fusion.2.info, bf16[256,2560]{1,0:T(8,128)(2,1)} %copy-done.6, bf16[256,2560]{1,0:T(8,128)(2,1)} %collective-permute-done.12.refs_1_, bf16[2,640,2560]{2,1,0:T(8,128)(2,1)} %bitcast.33, ...), custom_call_target="tpu_custom_call" | custom-call | flops 18454937600 | bytes 31457280 | tf_op jit(solution)/shard_map/pre/pallas_call | solution.py:204
  282.1 29.2 %pre.13 = (bf16[512,640]{1,0:T(8,128)(2,1)}, bf16[2048,640]{1,0:T(8,128)(2,1)}, bf16[2048,640]{1,0:T(8,128)(2,1)}, bf16[512,2560]{1,0:T(8,128)(2,1)}) custom-call(s32[2]{0:T(128)} %pad_add_fusion.1.info, bf16[256,2560]{1,0:T(8,128)(2,1)} %copy-done.5, ...), custom_call_target="tpu_custom_call", output_to_operand_aliasing={{1}: (13, {}), {2}: (14, {})} | custom-call | flops 18454937600 | bytes 31457280 | tf_op jit(solution)/shard_map/pre/pallas_call | solution.py:204
  312.9 29.6 %pre.14 = (bf16[512,640]{1,0:T(8,128)(2,1)}, bf16[2048,640]{1,0:T(8,128)(2,1)}, bf16[2048,640]{1,0:T(8,128)(2,1)}, bf16[512,2560]{1,0:T(8,128)(2,1)}) custom-call(s32[2]{0:T(128)} %pad_add_fusion.3.info, bf16[256,2560]{1,0:T(8,128)(2,1)} %collective-permute-done.11.refs_11_.refs_0_, ...), custom_call_target="tpu_custom_call", output_to_operand_aliasing={{1}: (13, {}), {2}: (14, {})} | custom-call | flops 18454937600 | bytes 31457280 | tf_op jit(solution)/shard_map/pre/pallas_call | solution.py:204
  342.6 18.4 %attn.9.refs_11_ = bf16[256,2560]{1,0:T(8,128)(2,1)} custom-call(bf16[8,1,256]{2,1,0:T(2,128)(2,1)} %constant.68.clone.qm_ref, f32[8,1,256]{2,1,0:T(1,128)} %constant.69.clone.om_ref, bf16[2048,640]{1,0:T(8,128)(2,1)} %get-tuple-element.67.k_hbm.refs_12_, bf16[2048,640]{1,0:T(8,128)(2,1)} %get-tuple-element.68.v_hbm.refs_13_, ...), custom_call_target="tpu_custom_call" | custom-call | flops 3825205248 | bytes 5242880 | tf_op jit(solution)/shard_map/attn/pallas_call | solution.py:328
  362.0 29.4 %pre.15 = (bf16[512,640]{1,0:T(8,128)(2,1)}, bf16[2048,640]{1,0:T(8,128)(2,1)}, bf16[2048,640]{1,0:T(8,128)(2,1)}, bf16[512,2560]{1,0:T(8,128)(2,1)}) custom-call(s32[2]{0:T(128)} %pad_add_fusion.info, bf16[256,2560]{1,0:T(8,128)(2,1)} %collective-permute-done.9.refs_11_.refs_0_, ...), custom_call_target="tpu_custom_call", output_to_operand_aliasing={{1}: (13, {}), {2}: (14, {})} | custom-call | flops 18454937600 | bytes 31457280 | tf_op jit(solution)/shard_map/pre/pallas_call | solution.py:204
  391.5 21.9 %attn.10.refs_4_ = bf16[256,2560]{1,0:T(8,128)(2,1)} custom-call(bf16[8,1,256]{2,1,0:T(2,128)(2,1)} %constant.68.clone.qm_ref, f32[8,1,256]{2,1,0:T(1,128)} %constant.69.clone.om_ref, bf16[2048,640]{1,0:T(8,128)(2,1)} %get-tuple-element.71.k_hbm, bf16[2048,640]{1,0:T(8,128)(2,1)} %get-tuple-element.72.v_hbm, bf16[2,640,2560]{2,1,0:T(8,128)(2,1)} %bitcast.57, ...), custom_call_target="tpu_custom_call" | custom-call | flops 3825205248 | bytes 5242880 | tf_op jit(solution)/shard_map/attn/pallas_call | solution.py:328
  415.5 20.3 %attn.11 = bf16[512,2560]{1,0:T(8,128)(2,1)} custom-call(bf16[8,1,256]{2,1,0:T(2,128)(2,1)} %constant.68.clone.qm_ref, f32[8,1,256]{2,1,0:T(1,128)} %constant.69.clone.om_ref, bf16[2048,640]{1,0:T(8,128)(2,1)} %get-tuple-element.71.k_hbm, bf16[2048,640]{1,0:T(8,128)(2,1)} %get-tuple-element.72.v_hbm, bf16[2,640,2560]{2,1,0:T(8,128)(2,1)} %bitcast.58, ...), custom_call_target="tpu_custom_call" | custom-call | flops 7650410496 | bytes 5242880 | tf_op jit(solution)/shard_map/attn/pallas_call | solution.py:328
  435.8 9.6 %collective-permute-done.16 = bf16[256,2560]{1,0:T(8,128)(2,1)} collective-permute-done((bf16[256,2560]{1,0:T(8,128)(2,1)}, bf16[256,2560]{1,0:T(8,128)(2,1)}, u32[]{:S(2)}, u32[]{:S(2)}) %collective-permute-start.16) | collective-permute-done | bytes 1310752 | tf_op jit(solution)/shard_map/ppermute | solution.py:365
  445.4 27.3 %collective-permute-done.15 = bf16[256,2560]{1,0:T(8,128)(2,1)} collective-permute-done((bf16[256,2560]{1,0:T(8,128)(2,1)S(1)}, bf16[256,2560]{1,0:T(8,128)(2,1)}, u32[]{:S(2)}, u32[]{:S(2)}) %collective-permute-start.15) | collective-permute-done | bytes 1310752 | tf_op jit(solution)/shard_map/ppermute | solution.py:365
  472.7 3.9 broadcast_select_fusion.1
  476.6 3.0 collective-permute-done.17
  (109 shorter events, 27.7 us)
Async XLA Ops:
  1.9 3.6 collective-permute-start
  12.6 11.1 %collective-permute-start.4 = (bf16[256,2560]{1,0:T(8,128)(2,1)}, bf16[256,2560]{1,0:T(8,128)(2,1)}, u32[]{:S(2)}, u32[]{:S(2)}) collective-permute-start(bf16[256,2560]{1,0:T(8,128)(2,1)} %get-tuple-element.105.refs_0_), channel_id=1, source_target_pairs={{0,1},{1,0},{2,3},{3,2},{4,5},{5,4},{6,7},{7,6}} | collective-permute-start | bytes 3932168 | tf_op jit(solution)/shard_map/ppermute | solution.py:368
  20.7 32.7 %collective-permute-start.3 = (bf16[256,2560]{1,0:T(8,128)(2,1)}, bf16[256,2560]{1,0:T(8,128)(2,1)}, u32[]{:S(2)}, u32[]{:S(2)}) collective-permute-start(bf16[256,2560]{1,0:T(8,128)(2,1)} %get-tuple-element.105.refs_0_), channel_id=1, source_target_pairs={{0,2},{1,3},{2,0},{3,1},{4,6},{5,7},{6,4},{7,5}} | collective-permute-start | bytes 3932168 | tf_op jit(solution)/shard_map/ppermute | solution.py:365
  23.3 30.2 %collective-permute-start.2 = (bf16[256,2560]{1,0:T(8,128)(2,1)}, bf16[256,2560]{1,0:T(8,128)(2,1)}, u32[]{:S(2)}, u32[]{:S(2)}) collective-permute-start(bf16[256,2560]{1,0:T(8,128)(2,1)} %get-tuple-element.104.refs_0_), channel_id=1, source_target_pairs={{0,1},{1,0},{2,3},{3,2},{4,5},{5,4},{6,7},{7,6}} | collective-permute-start | bytes 3932168 | tf_op jit(solution)/shard_map/ppermute | solution.py:368
  23.4 59.6 %collective-permute-start.1 = (bf16[256,2560]{1,0:T(8,128)(2,1)}, bf16[256,2560]{1,0:T(8,128)(2,1)}, u32[]{:S(2)}, u32[]{:S(2)}) collective-permute-start(bf16[256,2560]{1,0:T(8,128)(2,1)} %get-tuple-element.104.refs_0_), channel_id=1, source_target_pairs={{0,2},{1,3},{2,0},{3,1},{4,6},{5,7},{6,4},{7,5}} | collective-permute-start | bytes 3932168 | tf_op jit(solution)/shard_map/ppermute | solution.py:365
  53.4 30.0 %collective-permute-start.6 = (bf16[256,2560]{1,0:T(8,128)(2,1)}, bf16[256,2560]{1,0:T(8,128)(2,1)}, u32[]{:S(2)}, u32[]{:S(2)}) collective-permute-start(bf16[256,2560]{1,0:T(8,128)(2,1)} %collective-permute-done.3.refs_11_.refs_0_), channel_id=1, source_target_pairs={{0,1},{1,0},{2,3},{3,2},{4,5},{5,4},{6,7},{7,6}} | collective-permute-start | bytes 3932168 | tf_op jit(solution)/shard_map/ppermute | solution.py:368
  83.0 48.8 %collective-permute-start.5 = (bf16[256,2560]{1,0:T(8,128)(2,1)}, bf16[256,2560]{1,0:T(8,128)(2,1)}, u32[]{:S(2)}, u32[]{:S(2)}) collective-permute-start(bf16[256,2560]{1,0:T(8,128)(2,1)} %collective-permute-done.1.refs_11_.refs_0_), channel_id=1, source_target_pairs={{0,1},{1,0},{2,3},{3,2},{4,5},{5,4},{6,7},{7,6}} | collective-permute-start | bytes 3932168 | tf_op jit(solution)/shard_map/ppermute | solution.py:368
  161.2 23.8 %copy-start.12 = (bf16[2,2560]{1,0:T(2,128)(2,1)S(1)}, bf16[2,2560]{1,0:T(2,128)(2,1)}, u32[]{:S(2)}) copy-start(bf16[2,2560]{1,0:T(2,128)(2,1)} %param.31) | copy-start | bytes 30724
  161.2 23.8 %copy-start.13 = (bf16[2,2560]{1,0:T(2,128)(2,1)S(1)}, bf16[2,2560]{1,0:T(2,128)(2,1)}, u32[]{:S(2)}) copy-start(bf16[2,2560]{1,0:T(2,128)(2,1)} %param.27) | copy-start | bytes 30724
  183.0 32.0 %collective-permute-start.8 = (bf16[256,2560]{1,0:T(8,128)(2,1)}, bf16[256,2560]{1,0:T(8,128)(2,1)}, u32[]{:S(2)}, u32[]{:S(2)}) collective-permute-start(bf16[256,2560]{1,0:T(8,128)(2,1)} %attn.7.refs_4_), channel_id=1, source_target_pairs={{0,2},{1,3},{2,0},{3,1},{4,6},{5,7},{6,4},{7,5}} | collective-permute-start | bytes 3932168 | tf_op jit(solution)/shard_map/ppermute | solution.py:365
  183.0 59.3 %collective-permute-start.7 = (bf16[256,2560]{1,0:T(8,128)(2,1)}, bf16[256,2560]{1,0:T(8,128)(2,1)}, u32[]{:S(2)}, u32[]{:S(2)}) collective-permute-start(bf16[256,2560]{1,0:T(8,128)(2,1)} %attn.6.refs_11_), channel_id=1, source_target_pairs={{0,2},{1,3},{2,0},{3,1},{4,6},{5,7},{6,4},{7,5}} | collective-permute-start | bytes 3932168 | tf_op jit(solution)/shard_map/ppermute | solution.py:365
  248.9 33.0 %copy-start.5 = (bf16[256,2560]{1,0:T(8,128)(2,1)}, bf16[256,2560]{1,0:T(8,128)(2,1)S(1)}, u32[]{:S(2)}) copy-start(bf16[256,2560]{1,0:T(8,128)(2,1)S(1)} %get-tuple-element.102.refs_0_) | copy-start | bytes 3932164
  248.9 3.6 collective-permute-start.12
  250.3 31.8 %collective-permute-start.11 = (bf16[256,2560]{1,0:T(8,128)(2,1)S(1)}, bf16[256,2560]{1,0:T(8,128)(2,1)}, u32[]{:S(2)}, u32[]{:S(2)}) collective-permute-start(bf16[256,2560]{1,0:T(8,128)(2,1)S(1)} %get-tuple-element.103.refs_0_), channel_id=1, source_target_pairs={{0,2},{1,3},{2,0},{3,1},{4,6},{5,7},{6,4},{7,5}} | collective-permute-start | bytes 3932168 | tf_op jit(solution)/shard_map/ppermute | solution.py:365
  250.6 31.5 %collective-permute-start.10 = (bf16[256,2560]{1,0:T(8,128)(2,1)S(1)}, bf16[256,2560]{1,0:T(8,128)(2,1)}, u32[]{:S(2)}, u32[]{:S(2)}) collective-permute-start(bf16[256,2560]{1,0:T(8,128)(2,1)S(1)} %get-tuple-element.102.refs_0_), channel_id=1, source_target_pairs={{0,1},{1,0},{2,3},{3,2},{4,5},{5,4},{6,7},{7,6}} | collective-permute-start | bytes 3932168 | tf_op jit(solution)/shard_map/ppermute | solution.py:368
  250.7 60.6 %collective-permute-start.9 = (bf16[256,2560]{1,0:T(8,128)(2,1)S(1)}, bf16[256,2560]{1,0:T(8,128)(2,1)}, u32[]{:S(2)}, u32[]{:S(2)}) collective-permute-start(bf16[256,2560]{1,0:T(8,128)(2,1)S(1)} %get-tuple-element.102.refs_0_), channel_id=1, source_target_pairs={{0,2},{1,3},{2,0},{3,1},{4,6},{5,7},{6,4},{7,5}} | collective-permute-start | bytes 3932168 | tf_op jit(solution)/shard_map/ppermute | solution.py:365
  282.0 29.8 %collective-permute-start.14 = (bf16[256,2560]{1,0:T(8,128)(2,1)}, bf16[256,2560]{1,0:T(8,128)(2,1)S(1)}, u32[]{:S(2)}, u32[]{:S(2)}) collective-permute-start(bf16[256,2560]{1,0:T(8,128)(2,1)} %collective-permute-done.11.refs_11_.refs_0_), channel_id=1, source_target_pairs={{0,1},{1,0},{2,3},{3,2},{4,5},{5,4},{6,7},{7,6}} | collective-permute-start | bytes 3932168 | tf_op jit(solution)/shard_map/ppermute | solution.py:368
  311.3 49.7 %collective-permute-start.13 = (bf16[256,2560]{1,0:T(8,128)(2,1)}, bf16[256,2560]{1,0:T(8,128)(2,1)S(1)}, u32[]{:S(2)}, u32[]{:S(2)}) collective-permute-start(bf16[256,2560]{1,0:T(8,128)(2,1)} %collective-permute-done.9.refs_11_.refs_0_), channel_id=1, source_target_pairs={{0,1},{1,0},{2,3},{3,2},{4,5},{5,4},{6,7},{7,6}} | collective-permute-start | bytes 3932168 | tf_op jit(solution)/shard_map/ppermute | solution.py:368
  391.5 21.9 %copy-start.4 = (bf16[256,2560]{1,0:T(8,128)(2,1)S(1)}, bf16[256,2560]{1,0:T(8,128)(2,1)}, u32[]{:S(2)}) copy-start(bf16[256,2560]{1,0:T(8,128)(2,1)} %attn.9.refs_11_) | copy-start | bytes 3932164
  413.4 32.0 %collective-permute-start.16 = (bf16[256,2560]{1,0:T(8,128)(2,1)}, bf16[256,2560]{1,0:T(8,128)(2,1)}, u32[]{:S(2)}, u32[]{:S(2)}) collective-permute-start(bf16[256,2560]{1,0:T(8,128)(2,1)} %attn.10.refs_4_), channel_id=1, source_target_pairs={{0,2},{1,3},{2,0},{3,1},{4,6},{5,7},{6,4},{7,5}} | collective-permute-start | bytes 3932168 | tf_op jit(solution)/shard_map/ppermute | solution.py:365
  413.5 59.2 %collective-permute-start.15 = (bf16[256,2560]{1,0:T(8,128)(2,1)S(1)}, bf16[256,2560]{1,0:T(8,128)(2,1)}, u32[]{:S(2)}, u32[]{:S(2)}) collective-permute-start(bf16[256,2560]{1,0:T(8,128)(2,1)S(1)} %copy-done.4), channel_id=1, source_target_pairs={{0,2},{1,3},{2,0},{3,1},{4,6},{5,7},{6,4},{7,5}} | collective-permute-start | bytes 3932168 | tf_op jit(solution)/shard_map/ppermute | solution.py:365
  415.5 57.2 %copy-start.1 = (bf16[256,2560]{1,0:T(8,128)(2,1)S(1)}, bf16[256,2560]{1,0:T(8,128)(2,1)}, u32[]{:S(2)}) copy-start(bf16[256,2560]{1,0:T(8,128)(2,1)} %copy-done) | copy-start | bytes 3932164
  415.5 57.2 %copy-start.3 = (bf16[256,2560]{1,0:T(8,128)(2,1)S(1)}, bf16[256,2560]{1,0:T(8,128)(2,1)}, u32[]{:S(2)}) copy-start(bf16[256,2560]{1,0:T(8,128)(2,1)} %copy-done.2) | copy-start | bytes 3932164
  476.6 3.1 collective-permute-start.17
  (11 other events, 38.7 us)

commit v3 on v2

--- a/solution.py
+++ b/solution.py
@@ -92,9 +92,11 @@
         for s, row in enumerate((row0, row1)):
             xcopies.append(pltpu.make_async_copy(x_hbm[2 * p + s], x_s.at[pl.ds(p * ROWS + row, half)], x_sem.at[2 * p + s]))
     tcopies = [pltpu.make_async_copy(t.at[pl.ds(brow, R)], tab_s.at[s], x_sem.at[2 * n_pair + s]) for s, t in enumerate((cos_hbm, sin_hbm))]
-    pcopies = [[pltpu.make_async_copy(w.at[layer, pl.ds(src, n)], wp_s.at[pl.ds(s * N + dst, n)], p_sem.at[s])
-                for src, dst, n in unit_runs()] for s, w in enumerate((wq, wk))]
-    pcopies.append([pltpu.make_async_copy(wv.at[layer], wp_s.at[pl.ds(2 * N, N)], p_sem.at[2])])
+    pcopies = []
+    for s, w in enumerate((wq, wk)):
+        for src, dst, n in unit_runs():
+            pcopies.append(pltpu.make_async_copy(w.at[layer, pl.ds(src, n)], wp_s.at[pl.ds(s * N + dst, n)], p_sem.at[s]))
+    pcopies.append(pltpu.make_async_copy(wv.at[layer], wp_s.at[pl.ds(2 * N, N)], p_sem.at[2]))
     pwaits = [pltpu.make_async_copy(w.at[layer], wp_s.at[pl.ds(s * N, N)], p_sem.at[s]) for s, w in enumerate((wq, wk, wv))]
     kv_rows = pl.ds(brow, R)
     hcopies = [pltpu.make_async_copy(h_s.at[0], q_out, h_sem.at[0]),
@@ -102,11 +104,11 @@
                pltpu.make_async_copy(h_s.at[2], v_out.at[kv_rows], h_sem.at[2])]
 
     def tile_copy(w, t, slot):
-        return pltpu.make_async_copy(w.at[layer, :, pl.ds(t * bf, bf)], wt_s.at[slot], t_sem.at[slot])
+        return pltpu.make_async_copy(w.at[layer, :, pl.ds(pl.multiple_of(t * bf, bf), bf)], wt_s.at[slot], t_sem.at[slot])
 
     def out_copy(t):
-        slot = t % 2
-        return pltpu.make_async_copy(o_s.at[slot], mlp_out.at[:, pl.ds(t * bf, bf)], o_sem.at[slot])
+        slot = lax.rem(t, 2)
+        return pltpu.make_async_copy(o_s.at[slot], mlp_out.at[:, pl.ds(pl.multiple_of(t * bf, bf), bf)], o_sem.at[slot])
 
     def epilogue(r):
         step = 64
@@ -131,31 +133,45 @@
 
     def activate(t):
         step = 64
-        slot = t % 2
+        slot = lax.rem(t, 2)
         bias = bu_ref[t].astype(F32)
         for rr in range(0, R, step):
             u_s[t + 1, rr:rr + step, :] = gelu(z_s[slot, rr:rr + step, :] + bias).astype(BF16)
 
     def slot3(t):
-        return t % 3
+        return lax.rem(t, 3)
 
     for cp in xcopies:
         cp.start()
     tile_copy(wu, 0, 0).start()
+    tile_copy(wu, 1, 1).start()
+    for cp in pcopies + tcopies:
+        cp.start()
     for cp in xcopies:
         cp.wait()
 
     def up_tile(t, first):
         tile_copy(wu, t, slot3(t)).wait()
-        (tile_copy(wu, t + 1, slot3(t + 1)) if t + 1 < nf else tile_copy(wd, 0, slot3(nf))).start()
-        for cp in pcopies[t - 1] if 1 <= t <= 3 else tcopies if t == 0 else ():
-            cp.start()
-        z_s[t % 2] = jnp.dot(x_s[...], wt_s[slot3(t)], preferred_element_type=F32)
+        if isinstance(t, int):
+            (tile_copy(wu, t + 2, slot3(t + 2)) if t + 2 < nf else tile_copy(wd, t + 2 - nf, slot3(t + 2))).start()
+        else:
+            @pl.when(t + 2 < nf)
+            def _():
+                tile_copy(wu, t + 2, slot3(t + 2)).start()
+
+            @pl.when(t + 2 >= nf)
+            def _():
+                tile_copy(wd, t + 2 - nf, slot3(t + 2)).start()
+        z_s[lax.rem(t, 2)] = jnp.dot(x_s[...], wt_s[slot3(t)], preferred_element_type=F32)
         if not first:
             activate(t - 1)
 
-    for t in range(nf):
-        up_tile(t, t == 0)
+    if nr == 1:
+        for t in range(nf):
+            up_tile(t, t == 0)
+    else:
+        up_tile(0, True)
+        lax.fori_loop(1, nf, lambda t, c: (up_tile(t, False), c)[1], 0)
     for cp in pwaits + tcopies:
         cp.wait()
     for r in range(nr):
@@ -169,22 +185,35 @@
     def down_tile(t, first):
         slot = slot3(t + nf)
         tile_copy(wd, t, slot).wait()
-        if t + 1 < nf:
-            tile_copy(wd, t + 1, slot3(t + nf + 1)).start()
-        if t >= 2:
-            out_copy(t - 2).wait()
+        if isinstance(t, int):
+            if t + 2 < nf:
+                tile_copy(wd, t + 2, slot3(t + nf + 2)).start()
+            if t >= 2:
+                out_copy(t - 2).wait()
+        else:
+            @pl.when(t + 2 < nf)
+            def _():
+                tile_copy(wd, t + 2, slot3(t + nf + 2)).start()
+
+            @pl.when(t >= 2)
+            def _():
+                out_copy(t - 2).wait()
         u = jnp.concatenate([u_s[f + 1] for f in range(nf)], axis=1)
         o = jnp.dot(u, wt_s[slot], preferred_element_type=F32)
         if first:
             epilogue(nr - 1)
-        o_s[t % 2] = o.astype(BF16)
+        o_s[lax.rem(t, 2)] = o.astype(BF16)
         out_copy(t).start()
         if first:
             for cp in hcopies:
                 cp.start()
 
-    for t in range(nf):
-        down_tile(t, t == 0)
+    if nr == 1:
+        for t in range(nf):
+            down_tile(t, t == 0)
+    else:
+        down_tile(0, True)
+        lax.fori_loop(1, nf, lambda t, c: (down_tile(t, False), c)[1], 0)
     out_copy(nf - 2).wait()
     out_copy(nf - 1).wait()
     for cp in hcopies:

time: 488 us -> 485 us (level)
  transfers between devices with their start and end apart: 18 -> 18, of which waited for: 7 -> 8; matrix products, arithmetic and copies ran while one was open for 2% -> 2% of each run, Pallas kernels for 53% -> 53%
where the time goes in v3:
time: 485 us; the launch traced here: 479 us
  Pallas kernels  353 us (73%)
  waiting for transfers between devices  78.9 us (16%)
  other arithmetic  28.9 us (6%)
  starting transfers between devices  11.6 us (2%)
  local copies, waits for them, and re-layouts  5.45 us (1%)
    pallas_call x8, Pallas kernels, pre(): pl.pallas_call(functools.partial(pre_kernel, nf, layer, n_pair, len(after...  232 us
    pallas_call x6, Pallas kernels, attn(): pl.pallas_call(functools.partial(attn_kernel, layer, bases, own, n_blocks...  121 us
    ppermute x8, waiting for transfers between devices, to_chip(): return lax.ppermute(a, 'tp', across)  74.9 us
  transfers between devices with their start and end apart: 18, of which 8 were waited for; matrix products, arithmetic and copies ran while one was open for 2% of the time, Pallas kernels for 53%

profile of v3, /device:TPU:0, one launch (start us, length us, event | category | flops | bytes accessed | tf_op | source)
XLA Modules:
  0.0 478.6 jit_solution(5247211157994285569)
XLA Ops:
  5.6 3.6 convert_reduce_fusion.2
  15.0 5.0 %fusion.40 = (f32[2048,128]{1,0:T(8,128)}, f32[2048,128]{1,0:T(8,128)}) fusion(f32[128]{0:T(128)S(1)} %fusion.45), kind=kLoop, calls=%fused_computation.62 | loop fusion | flops 262144 | bytes 2097664 | tf_op jit(solution)/shard_map/sin | solution.py:375
  20.7 2.6 collective-permute-start.3
  23.7 29.1 %pre.8 = (bf16[512,640]{1,0:T(8,128)(2,1)}, bf16[2048,640]{1,0:T(8,128)(2,1)}, bf16[2048,640]{1,0:T(8,128)(2,1)}, bf16[512,2560]{1,0:T(8,128)(2,1)}) custom-call(s32[2]{0:T(128)} %pad_add_fusion.2.info, bf16[256,2560]{1,0:T(8,128)(2,1)} %get-tuple-element.105.refs_0_, bf16[256,2560]{1,0:T(8,128)(2,1)} %collective-permute-done.4.refs_1_, ...), custom_call_target="tpu_custom_call" | custom-call | flops 18454937600 | bytes 31457280 | tf_op jit(solution)/shard_map/pre/pallas_call | solution.py:233
  53.3 28.9 %pre.9 = (bf16[512,640]{1,0:T(8,128)(2,1)}, bf16[2048,640]{1,0:T(8,128)(2,1)}, bf16[2048,640]{1,0:T(8,128)(2,1)}, bf16[512,2560]{1,0:T(8,128)(2,1)}) custom-call(s32[2]{0:T(128)} %pad_add_fusion.1.info, bf16[256,2560]{1,0:T(8,128)(2,1)} %get-tuple-element.104.refs_0_, ...), custom_call_target="tpu_custom_call", output_to_operand_aliasing={{1}: (13, {}), {2}: (14, {})} | custom-call | flops 18454937600 | bytes 31457280 | tf_op jit(solution)/shard_map/pre/pallas_call | solution.py:233
  82.7 28.8 %pre.10 = (bf16[512,640]{1,0:T(8,128)(2,1)}, bf16[2048,640]{1,0:T(8,128)(2,1)}, bf16[2048,640]{1,0:T(8,128)(2,1)}, bf16[512,2560]{1,0:T(8,128)(2,1)}) custom-call(s32[2]{0:T(128)} %pad_add_fusion.3.info, bf16[256,2560]{1,0:T(8,128)(2,1)} %collective-permute-done.3.refs_11_.refs_0_, ...), custom_call_target="tpu_custom_call", output_to_operand_aliasing={{1}: (13, {}), {2}: (14, {})} | custom-call | flops 18454937600 | bytes 31457280 | tf_op jit(solution)/shard_map/pre/pallas_call | solution.py:233
  111.5 18.9 %attn.6.refs_11_ = bf16[256,2560]{1,0:T(8,128)(2,1)} custom-call(bf16[8,1,256]{2,1,0:T(2,128)(2,1)} %constant.68.clone.qm_ref, f32[8,1,256]{2,1,0:T(1,128)} %constant.69.clone.om_ref, bf16[2048,640]{1,0:T(8,128)(2,1)} %get-tuple-element.49.k_hbm.refs_12_, bf16[2048,640]{1,0:T(8,128)(2,1)} %get-tuple-element.50.v_hbm.refs_13_, ...), custom_call_target="tpu_custom_call" | custom-call | flops 3825205248 | bytes 5242880 | tf_op jit(solution)/shard_map/attn/pallas_call | solution.py:357
  130.4 28.8 %pre.11 = (bf16[512,640]{1,0:T(8,128)(2,1)}, bf16[2048,640]{1,0:T(8,128)(2,1)}, bf16[2048,640]{1,0:T(8,128)(2,1)}, bf16[512,2560]{1,0:T(8,128)(2,1)}) custom-call(s32[2]{0:T(128)} %pad_add_fusion.info, bf16[256,2560]{1,0:T(8,128)(2,1)} %collective-permute-done.1.refs_11_.refs_0_, ...), custom_call_target="tpu_custom_call", output_to_operand_aliasing={{1}: (13, {}), {2}: (14, {})} | custom-call | flops 18454937600 | bytes 31457280 | tf_op jit(solution)/shard_map/pre/pallas_call | solution.py:233
  159.3 21.8 %attn.7.refs_4_ = bf16[256,2560]{1,0:T(8,128)(2,1)} custom-call(bf16[8,1,256]{2,1,0:T(2,128)(2,1)} %constant.68.clone.qm_ref, f32[8,1,256]{2,1,0:T(1,128)} %constant.69.clone.om_ref, bf16[2048,640]{1,0:T(8,128)(2,1)} %get-tuple-element.53.k_hbm, bf16[2048,640]{1,0:T(8,128)(2,1)} %get-tuple-element.54.v_hbm, bf16[2,640,2560]{2,1,0:T(8,128)(2,1)} %bitcast.54, ...), custom_call_target="tpu_custom_call" | custom-call | flops 3825205248 | bytes 5242880 | tf_op jit(solution)/shard_map/attn/pallas_call | solution.py:357
  183.2 20.2 %attn.8 = bf16[512,2560]{1,0:T(8,128)(2,1)} custom-call(bf16[8,1,256]{2,1,0:T(2,128)(2,1)} %constant.68.clone.qm_ref, f32[8,1,256]{2,1,0:T(1,128)} %constant.69.clone.om_ref, bf16[2048,640]{1,0:T(8,128)(2,1)} %get-tuple-element.53.k_hbm, bf16[2048,640]{1,0:T(8,128)(2,1)} %get-tuple-element.54.v_hbm, bf16[2,640,2560]{2,1,0:T(8,128)(2,1)} %bitcast.55, ...), custom_call_target="tpu_custom_call" | custom-call | flops 7650410496 | bytes 5242880 | tf_op jit(solution)/shard_map/attn/pallas_call | solution.py:357
  203.5 9.6 %collective-permute-done.8 = bf16[256,2560]{1,0:T(8,128)(2,1)} collective-permute-done((bf16[256,2560]{1,0:T(8,128)(2,1)}, bf16[256,2560]{1,0:T(8,128)(2,1)}, u32[]{:S(2)}, u32[]{:S(2)}) %collective-permute-start.8) | collective-permute-done | bytes 1310752 | tf_op jit(solution)/shard_map/ppermute | solution.py:394
  213.1 27.3 %collective-permute-done.7 = bf16[256,2560]{1,0:T(8,128)(2,1)} collective-permute-done((bf16[256,2560]{1,0:T(8,128)(2,1)}, bf16[256,2560]{1,0:T(8,128)(2,1)}, u32[]{:S(2)}, u32[]{:S(2)}) %collective-permute-start.7) | collective-permute-done | bytes 1310752 | tf_op jit(solution)/shard_map/ppermute | solution.py:394
  240.3 4.2 convert_reduce_fusion
  250.4 28.8 %pre.12 = (bf16[512,640]{1,0:T(8,128)(2,1)}, bf16[2048,640]{1,0:T(8,128)(2,1)}, bf16[2048,640]{1,0:T(8,128)(2,1)}, bf16[512,2560]{1,0:T(8,128)(2,1)}) custom-call(s32[2]{0:T(128)} %pad_add_fusion.2.info, bf16[256,2560]{1,0:T(8,128)(2,1)} %copy-done.6, bf16[256,2560]{1,0:T(8,128)(2,1)} %collective-permute-done.12.refs_1_, bf16[2,640,2560]{2,1,0:T(8,128)(2,1)} %bitcast.33, ...), custom_call_target="tpu_custom_call" | custom-call | flops 18454937600 | bytes 31457280 | tf_op jit(solution)/shard_map/pre/pallas_call | solution.py:233
  280.1 29.3 %pre.13 = (bf16[512,640]{1,0:T(8,128)(2,1)}, bf16[2048,640]{1,0:T(8,128)(2,1)}, bf16[2048,640]{1,0:T(8,128)(2,1)}, bf16[512,2560]{1,0:T(8,128)(2,1)}) custom-call(s32[2]{0:T(128)} %pad_add_fusion.1.info, bf16[256,2560]{1,0:T(8,128)(2,1)} %copy-done.5, ...), custom_call_target="tpu_custom_call", output_to_operand_aliasing={{1}: (13, {}), {2}: (14, {})} | custom-call | flops 18454937600 | bytes 31457280 | tf_op jit(solution)/shard_map/pre/pallas_call | solution.py:233
  311.0 28.8 %pre.14 = (bf16[512,640]{1,0:T(8,128)(2,1)}, bf16[2048,640]{1,0:T(8,128)(2,1)}, bf16[2048,640]{1,0:T(8,128)(2,1)}, bf16[512,2560]{1,0:T(8,128)(2,1)}) custom-call(s32[2]{0:T(128)} %pad_add_fusion.3.info, bf16[256,2560]{1,0:T(8,128)(2,1)} %collective-permute-done.11.refs_11_.refs_0_, ...), custom_call_target="tpu_custom_call", output_to_operand_aliasing={{1}: (13, {}), {2}: (14, {})} | custom-call | flops 18454937600 | bytes 31457280 | tf_op jit(solution)/shard_map/pre/pallas_call | solution.py:233
  339.9 18.4 %attn.9.refs_11_ = bf16[256,2560]{1,0:T(8,128)(2,1)} custom-call(bf16[8,1,256]{2,1,0:T(2,128)(2,1)} %constant.68.clone.qm_ref, f32[8,1,256]{2,1,0:T(1,128)} %constant.69.clone.om_ref, bf16[2048,640]{1,0:T(8,128)(2,1)} %get-tuple-element.67.k_hbm.refs_12_, bf16[2048,640]{1,0:T(8,128)(2,1)} %get-tuple-element.68.v_hbm.refs_13_, ...), custom_call_target="tpu_custom_call" | custom-call | flops 3825205248 | bytes 5242880 | tf_op jit(solution)/shard_map/attn/pallas_call | solution.py:357
  359.4 28.9 %pre.15 = (bf16[512,640]{1,0:T(8,128)(2,1)}, bf16[2048,640]{1,0:T(8,128)(2,1)}, bf16[2048,640]{1,0:T(8,128)(2,1)}, bf16[512,2560]{1,0:T(8,128)(2,1)}) custom-call(s32[2]{0:T(128)} %pad_add_fusion.info, bf16[256,2560]{1,0:T(8,128)(2,1)} %collective-permute-done.9.refs_11_.refs_0_, ...), custom_call_target="tpu_custom_call", output_to_operand_aliasing={{1}: (13, {}), {2}: (14, {})} | custom-call | flops 18454937600 | bytes 31457280 | tf_op jit(solution)/shard_map/pre/pallas_call | solution.py:233
  388.3 21.9 %attn.10.refs_4_ = bf16[256,2560]{1,0:T(8,128)(2,1)} custom-call(bf16[8,1,256]{2,1,0:T(2,128)(2,1)} %constant.68.clone.qm_ref, f32[8,1,256]{2,1,0:T(1,128)} %constant.69.clone.om_ref, bf16[2048,640]{1,0:T(8,128)(2,1)} %get-tuple-element.71.k_hbm, bf16[2048,640]{1,0:T(8,128)(2,1)} %get-tuple-element.72.v_hbm, bf16[2,640,2560]{2,1,0:T(8,128)(2,1)} %bitcast.57, ...), custom_call_target="tpu_custom_call" | custom-call | flops 3825205248 | bytes 5242880 | tf_op jit(solution)/shard_map/attn/pallas_call | solution.py:357
  412.2 20.3 %attn.11 = bf16[512,2560]{1,0:T(8,128)(2,1)} custom-call(bf16[8,1,256]{2,1,0:T(2,128)(2,1)} %constant.68.clone.qm_ref, f32[8,1,256]{2,1,0:T(1,128)} %constant.69.clone.om_ref, bf16[2048,640]{1,0:T(8,128)(2,1)} %get-tuple-element.71.k_hbm, bf16[2048,640]{1,0:T(8,128)(2,1)} %get-tuple-element.72.v_hbm, bf16[2,640,2560]{2,1,0:T(8,128)(2,1)} %bitcast.58, ...), custom_call_target="tpu_custom_call" | custom-call | flops 7650410496 | bytes 5242880 | tf_op jit(solution)/shard_map/attn/pallas_call | solution.py:357
  432.6 9.6 %collective-permute-done.16 = bf16[256,2560]{1,0:T(8,128)(2,1)} collective-permute-done((bf16[256,2560]{1,0:T(8,128)(2,1)}, bf16[256,2560]{1,0:T(8,128)(2,1)}, u32[]{:S(2)}, u32[]{:S(2)}) %collective-permute-start.16) | collective-permute-done | bytes 1310752 | tf_op jit(solution)/shard_map/ppermute | solution.py:394
  442.2 27.3 %collective-permute-done.15 = bf16[256,2560]{1,0:T(8,128)(2,1)} collective-permute-done((bf16[256,2560]{1,0:T(8,128)(2,1)S(1)}, bf16[256,2560]{1,0:T(8,128)(2,1)}, u32[]{:S(2)}, u32[]{:S(2)}) %collective-permute-start.15) | collective-permute-done | bytes 1310752 | tf_op jit(solution)/shard_map/ppermute | solution.py:394
  469.5 3.9 broadcast_select_fusion.1
  473.4 3.0 collective-permute-done.17
  (109 shorter events, 28.7 us)
Async XLA Ops:
  1.9 3.6 collective-permute-start
  12.6 11.1 %collective-permute-start.4 = (bf16[256,2560]{1,0:T(8,128)(2,1)}, bf16[256,2560]{1,0:T(8,128)(2,1)}, u32[]{:S(2)}, u32[]{:S(2)}) collective-permute-start(bf16[256,2560]{1,0:T(8,128)(2,1)} %get-tuple-element.105.refs_0_), channel_id=1, source_target_pairs={{0,1},{1,0},{2,3},{3,2},{4,5},{5,4},{6,7},{7,6}} | collective-permute-start | bytes 3932168 | tf_op jit(solution)/shard_map/ppermute | solution.py:397
  20.7 32.6 %collective-permute-start.3 = (bf16[256,2560]{1,0:T(8,128)(2,1)}, bf16[256,2560]{1,0:T(8,128)(2,1)}, u32[]{:S(2)}, u32[]{:S(2)}) collective-permute-start(bf16[256,2560]{1,0:T(8,128)(2,1)} %get-tuple-element.105.refs_0_), channel_id=1, source_target_pairs={{0,2},{1,3},{2,0},{3,1},{4,6},{5,7},{6,4},{7,5}} | collective-permute-start | bytes 3932168 | tf_op jit(solution)/shard_map/ppermute | solution.py:394
  23.3 29.9 %collective-permute-start.2 = (bf16[256,2560]{1,0:T(8,128)(2,1)}, bf16[256,2560]{1,0:T(8,128)(2,1)}, u32[]{:S(2)}, u32[]{:S(2)}) collective-permute-start(bf16[256,2560]{1,0:T(8,128)(2,1)} %get-tuple-element.104.refs_0_), channel_id=1, source_target_pairs={{0,1},{1,0},{2,3},{3,2},{4,5},{5,4},{6,7},{7,6}} | collective-permute-start | bytes 3932168 | tf_op jit(solution)/shard_map/ppermute | solution.py:397
  23.4 58.7 %collective-permute-start.1 = (bf16[256,2560]{1,0:T(8,128)(2,1)}, bf16[256,2560]{1,0:T(8,128)(2,1)}, u32[]{:S(2)}, u32[]{:S(2)}) collective-permute-start(bf16[256,2560]{1,0:T(8,128)(2,1)} %get-tuple-element.104.refs_0_), channel_id=1, source_target_pairs={{0,2},{1,3},{2,0},{3,1},{4,6},{5,7},{6,4},{7,5}} | collective-permute-start | bytes 3932168 | tf_op jit(solution)/shard_map/ppermute | solution.py:394
  53.3 29.4 %collective-permute-start.6 = (bf16[256,2560]{1,0:T(8,128)(2,1)}, bf16[256,2560]{1,0:T(8,128)(2,1)}, u32[]{:S(2)}, u32[]{:S(2)}) collective-permute-start(bf16[256,2560]{1,0:T(8,128)(2,1)} %collective-permute-done.3.refs_11_.refs_0_), channel_id=1, source_target_pairs={{0,1},{1,0},{2,3},{3,2},{4,5},{5,4},{6,7},{7,6}} | collective-permute-start | bytes 3932168 | tf_op jit(solution)/shard_map/ppermute | solution.py:397
  82.1 48.3 %collective-permute-start.5 = (bf16[256,2560]{1,0:T(8,128)(2,1)}, bf16[256,2560]{1,0:T(8,128)(2,1)}, u32[]{:S(2)}, u32[]{:S(2)}) collective-permute-start(bf16[256,2560]{1,0:T(8,128)(2,1)} %collective-permute-done.1.refs_11_.refs_0_), channel_id=1, source_target_pairs={{0,1},{1,0},{2,3},{3,2},{4,5},{5,4},{6,7},{7,6}} | collective-permute-start | bytes 3932168 | tf_op jit(solution)/shard_map/ppermute | solution.py:397
  159.2 23.9 %copy-start.12 = (bf16[2,2560]{1,0:T(2,128)(2,1)S(1)}, bf16[2,2560]{1,0:T(2,128)(2,1)}, u32[]{:S(2)}) copy-start(bf16[2,2560]{1,0:T(2,128)(2,1)} %param.31) | copy-start | bytes 30724
  159.3 23.9 %copy-start.13 = (bf16[2,2560]{1,0:T(2,128)(2,1)S(1)}, bf16[2,2560]{1,0:T(2,128)(2,1)}, u32[]{:S(2)}) copy-start(bf16[2,2560]{1,0:T(2,128)(2,1)} %param.27) | copy-start | bytes 30724
  181.1 32.0 %collective-permute-start.8 = (bf16[256,2560]{1,0:T(8,128)(2,1)}, bf16[256,2560]{1,0:T(8,128)(2,1)}, u32[]{:S(2)}, u32[]{:S(2)}) collective-permute-start(bf16[256,2560]{1,0:T(8,128)(2,1)} %attn.7.refs_4_), channel_id=1, source_target_pairs={{0,2},{1,3},{2,0},{3,1},{4,6},{5,7},{6,4},{7,5}} | collective-permute-start | bytes 3932168 | tf_op jit(solution)/shard_map/ppermute | solution.py:394
  181.1 59.2 %collective-permute-start.7 = (bf16[256,2560]{1,0:T(8,128)(2,1)}, bf16[256,2560]{1,0:T(8,128)(2,1)}, u32[]{:S(2)}, u32[]{:S(2)}) collective-permute-start(bf16[256,2560]{1,0:T(8,128)(2,1)} %attn.6.refs_11_), channel_id=1, source_target_pairs={{0,2},{1,3},{2,0},{3,1},{4,6},{5,7},{6,4},{7,5}} | collective-permute-start | bytes 3932168 | tf_op jit(solution)/shard_map/ppermute | solution.py:394
  246.9 32.4 %copy-start.5 = (bf16[256,2560]{1,0:T(8,128)(2,1)}, bf16[256,2560]{1,0:T(8,128)(2,1)S(1)}, u32[]{:S(2)}) copy-start(bf16[256,2560]{1,0:T(8,128)(2,1)S(1)} %get-tuple-element.102.refs_0_) | copy-start | bytes 3932164
  246.9 3.6 collective-permute-start.12
  248.3 31.8 %collective-permute-start.11 = (bf16[256,2560]{1,0:T(8,128)(2,1)S(1)}, bf16[256,2560]{1,0:T(8,128)(2,1)}, u32[]{:S(2)}, u32[]{:S(2)}) collective-permute-start(bf16[256,2560]{1,0:T(8,128)(2,1)S(1)} %get-tuple-element.103.refs_0_), channel_id=1, source_target_pairs={{0,2},{1,3},{2,0},{3,1},{4,6},{5,7},{6,4},{7,5}} | collective-permute-start | bytes 3932168 | tf_op jit(solution)/shard_map/ppermute | solution.py:394
  248.6 31.5 %collective-permute-start.10 = (bf16[256,2560]{1,0:T(8,128)(2,1)S(1)}, bf16[256,2560]{1,0:T(8,128)(2,1)}, u32[]{:S(2)}, u32[]{:S(2)}) collective-permute-start(bf16[256,2560]{1,0:T(8,128)(2,1)S(1)} %get-tuple-element.102.refs_0_), channel_id=1, source_target_pairs={{0,1},{1,0},{2,3},{3,2},{4,5},{5,4},{6,7},{7,6}} | collective-permute-start | bytes 3932168 | tf_op jit(solution)/shard_map/ppermute | solution.py:397
  248.7 60.7 %collective-permute-start.9 = (bf16[256,2560]{1,0:T(8,128)(2,1)S(1)}, bf16[256,2560]{1,0:T(8,128)(2,1)}, u32[]{:S(2)}, u32[]{:S(2)}) collective-permute-start(bf16[256,2560]{1,0:T(8,128)(2,1)S(1)} %get-tuple-element.102.refs_0_), channel_id=1, source_target_pairs={{0,2},{1,3},{2,0},{3,1},{4,6},{5,7},{6,4},{7,5}} | collective-permute-start | bytes 3932168 | tf_op jit(solution)/shard_map/ppermute | solution.py:394
  280.1 29.9 %collective-permute-start.14 = (bf16[256,2560]{1,0:T(8,128)(2,1)}, bf16[256,2560]{1,0:T(8,128)(2,1)S(1)}, u32[]{:S(2)}, u32[]{:S(2)}) collective-permute-start(bf16[256,2560]{1,0:T(8,128)(2,1)} %collective-permute-done.11.refs_11_.refs_0_), channel_id=1, source_target_pairs={{0,1},{1,0},{2,3},{3,2},{4,5},{5,4},{6,7},{7,6}} | collective-permute-start | bytes 3932168 | tf_op jit(solution)/shard_map/ppermute | solution.py:397
  309.4 48.9 %collective-permute-start.13 = (bf16[256,2560]{1,0:T(8,128)(2,1)}, bf16[256,2560]{1,0:T(8,128)(2,1)S(1)}, u32[]{:S(2)}, u32[]{:S(2)}) collective-permute-start(bf16[256,2560]{1,0:T(8,128)(2,1)} %collective-permute-done.9.refs_11_.refs_0_), channel_id=1, source_target_pairs={{0,1},{1,0},{2,3},{3,2},{4,5},{5,4},{6,7},{7,6}} | collective-permute-start | bytes 3932168 | tf_op jit(solution)/shard_map/ppermute | solution.py:397
  388.3 21.9 %copy-start.4 = (bf16[256,2560]{1,0:T(8,128)(2,1)S(1)}, bf16[256,2560]{1,0:T(8,128)(2,1)}, u32[]{:S(2)}) copy-start(bf16[256,2560]{1,0:T(8,128)(2,1)} %attn.9.refs_11_) | copy-start | bytes 3932164
  410.2 32.0 %collective-permute-start.16 = (bf16[256,2560]{1,0:T(8,128)(2,1)}, bf16[256,2560]{1,0:T(8,128)(2,1)}, u32[]{:S(2)}, u32[]{:S(2)}) collective-permute-start(bf16[256,2560]{1,0:T(8,128)(2,1)} %attn.10.refs_4_), channel_id=1, source_target_pairs={{0,2},{1,3},{2,0},{3,1},{4,6},{5,7},{6,4},{7,5}} | collective-permute-start | bytes 3932168 | tf_op jit(solution)/shard_map/ppermute | solution.py:394
  410.2 59.2 %collective-permute-start.15 = (bf16[256,2560]{1,0:T(8,128)(2,1)S(1)}, bf16[256,2560]{1,0:T(8,128)(2,1)}, u32[]{:S(2)}, u32[]{:S(2)}) collective-permute-start(bf16[256,2560]{1,0:T(8,128)(2,1)S(1)} %copy-done.4), channel_id=1, source_target_pairs={{0,2},{1,3},{2,0},{3,1},{4,6},{5,7},{6,4},{7,5}} | collective-permute-start | bytes 3932168 | tf_op jit(solution)/shard_map/ppermute | solution.py:394
  412.2 57.2 %copy-start.1 = (bf16[256,2560]{1,0:T(8,128)(2,1)S(1)}, bf16[256,2560]{1,0:T(8,128)(2,1)}, u32[]{:S(2)}) copy-start(bf16[256,2560]{1,0:T(8,128)(2,1)} %copy-done) | copy-start | bytes 3932164
  412.2 57.2 %copy-start.3 = (bf16[256,2560]{1,0:T(8,128)(2,1)S(1)}, bf16[256,2560]{1,0:T(8,128)(2,1)}, u32[]{:S(2)}) copy-start(bf16[256,2560]{1,0:T(8,128)(2,1)} %copy-done.2) | copy-start | bytes 3932164
  473.4 3.1 collective-permute-start.17
  (11 other events, 38.7 us)
